TPU v7x, 32 devices: a whole 2x2x4 slice. The times are simulated.
32 devices in a mesh: client: 32 (over z, y, x, core).
Axes of the slice: x: 2, y: 2, z: 4, core: 2. Of those that a mesh axis runs over, the one named last changes fastest.
Arguments:
- patches: bfloat16 [4096, 192], P('client'), may hold values from -6 to 6
- labels: int32 [256], replicated, may hold values from 0 to 9
- assign: int32 [32, 1], replicated, may hold values from 0 to 15; in each aligned block of 32 rows (0 to 31, 32 to 63, ...) at most 4 rows name the same one
- patch_embed: bfloat16 [192, 384], replicated, may hold values from -0.4375 to 0.4375
- positions: bfloat16 [16, 384], replicated, may hold values from -3 to 3
- client_in: bfloat16 [384, 3072], replicated, may hold values from -3 to 3
- client_down: bfloat16 [1536, 384], replicated, may hold values from -0.15625 to 0.15625
- server_in: bfloat16 [2, 6144, 3072], P(None, 'client'), may hold values from -3 to 3
- server_down: bfloat16 [2, 24576, 384], P(None, 'client'), may hold values from -0.15625 to 0.15625
- classifier: bfloat16 [16, 384, 10], replicated, may hold values from -15 to 15
Outputs:
- losses: float32 [32, 16], P('client')
- grad_patch_embed: float32 [192, 384], P(None, 'client')
- grad_positions: float32 [16, 384], P(None, 'client')
- grad_client_in: float32 [384, 3072], P(None, 'client')
- grad_client_down: float32 [1536, 384], P(None, 'client')
- grad_server_in: float32 [2, 6144, 3072], P(None, 'client')
- grad_server_down: float32 [2, 24576, 384], P(None, 'client')
- grad_classifier: float32 [6144, 10], P('client')
Inputs may be any that keep to these rules, and one draw needn't show every extreme that they name: `assign`: no server shard is named by more than 4 clients, a bound that some block reaches.
All inputs are finite; a program needn't handle non-finite values.
Results may differ from a plain program's by a relative error of at most 0.025.
Values may be sent and summed in bfloat16 or wider, within the bound.
A program may use at most 128 MiB of HBM per device.

v0:
```python
import functools
import math

import jax
import jax.numpy as jnp
from jax import lax
from jax.experimental import pallas as pl
from jax.experimental.pallas import tpu as pltpu
from jax.sharding import PartitionSpec as P

HEADS = 6
TOK = 16
IMG = 8
SHARDS = 16
SLOTS = 2
EPSILON = 1e-06
LANES = 128
PAD = 16
BF = jnp.bfloat16
F32 = jnp.float32
HIGH = lax.Precision.HIGHEST
GELU_C = math.sqrt(2.0 / math.pi)
VMEM_LIMIT = 60 * 1024 * 1024
MESH = pl.DeviceIdType.MESH


def mm(a, b, precision=None):
    return lax.dot_general(
        a, b, (((1,), (0,)), ((), ())), precision=precision, preferred_element_type=F32
    )


def mm_nt(a, b, precision=None):
    return lax.dot_general(
        a, b, (((1,), (1,)), ((), ())), precision=precision, preferred_element_type=F32
    )


def mm_tn(a, b):
    return lax.dot_general(a, b, (((0,), (0,)), ((), ())), preferred_element_type=F32)


def norm(v):
    centre = v - jnp.mean(v, axis=-1, keepdims=True)
    scale = lax.rsqrt(jnp.mean(centre * centre, axis=-1, keepdims=True) + EPSILON)
    return centre * scale, scale


def norm_back(normed, scale, grad):
    return scale * (
        grad
        - jnp.mean(grad, axis=-1, keepdims=True)
        - normed * jnp.mean(grad * normed, axis=-1, keepdims=True)
    )


def gelu(v):
    t = jnp.tanh(GELU_C * (v + 0.044715 * (v * v * v)))
    return 0.5 * v * (1.0 + t)


def gelu_both(v):
    sq = v * v
    t = jnp.tanh(GELU_C * (v + 0.044715 * (sq * v)))
    value = 0.5 * v * (1.0 + t)
    slope = 0.5 * (1.0 + t) + 0.5 * v * (1.0 - t * t) * (GELU_C * (1.0 + 0.134145 * sq))
    return value, slope


def image_mask():
    row = lax.broadcasted_iota(jnp.int32, (LANES, LANES), 0)
    col = lax.broadcasted_iota(jnp.int32, (LANES, LANES), 1)
    return row // TOK == col // TOK


def lane_masks(head_dim):
    lane = lax.broadcasted_iota(jnp.int32, (LANES, LANES), 1)
    return [lane // head_dim == h for h in range(LANES // head_dim)]


def attend(qkv_ref, probs_ref, att_ref, width):
    rows = qkv_ref.shape[0]
    head_dim = width // HEADS
    per = LANES // head_dim
    inside = image_mask()
    keeps = lane_masks(head_dim)
    for group in range(rows // LANES):
        r = slice(group * LANES, (group + 1) * LANES)
        for pair in range(width // LANES):
            lo = pair * LANES
            q = qkv_ref[r, lo : lo + LANES]
            k = qkv_ref[r, width + lo : width + lo + LANES]
            v = qkv_ref[r, 2 * width + lo : 2 * width + lo + LANES]
            out = jnp.zeros((LANES, LANES), F32)
            for h in range(per):
                s = mm_nt(jnp.where(keeps[h], q, 0.0), k, HIGH) * (1.0 / math.sqrt(head_dim))
                s = jnp.where(inside, s, -1e30)
                e = jnp.exp(s - jnp.max(s, axis=-1, keepdims=True))
                p = (e / jnp.sum(e, axis=-1, keepdims=True)).astype(BF)
                probs_ref[group * HEADS + pair * per + h] = p
                out = out + mm(p, jnp.where(keeps[h], v, 0.0).astype(BF))
            att_ref[r, lo : lo + LANES] = out.astype(BF)


def attend_back(grad, qkv_ref, probs_ref, dqkv_ref, width):
    rows = qkv_ref.shape[0]
    head_dim = width // HEADS
    per = LANES // head_dim
    keeps = lane_masks(head_dim)
    for group in range(rows // LANES):
        r = slice(group * LANES, (group + 1) * LANES)
        for pair in range(width // LANES):
            lo = pair * LANES
            q = qkv_ref[r, lo : lo + LANES]
            k = qkv_ref[r, width + lo : width + lo + LANES]
            v = qkv_ref[r, 2 * width + lo : 2 * width + lo + LANES].astype(BF)
            go = grad[r, lo : lo + LANES]
            dq = jnp.zeros((LANES, LANES), F32)
            dk = jnp.zeros((LANES, LANES), F32)
            dv = jnp.zeros((LANES, LANES), F32)
            for h in range(per):
                p = probs_ref[group * HEADS + pair * per + h]
                goh = jnp.where(keeps[h], go, 0.0).astype(BF)
                dp = mm_nt(goh, v)
                dv = dv + mm_tn(p, goh)
                pf = p.astype(F32)
                ds = pf * (dp - jnp.sum(pf * dp, axis=-1, keepdims=True))
                ds = (ds * (1.0 / math.sqrt(head_dim))).astype(BF)
                dq = dq + mm(ds, jnp.where(keeps[h], k, 0.0).astype(BF))
                dk = dk + mm_tn(ds, jnp.where(keeps[h], q, 0.0).astype(BF))
            dqkv_ref[r, lo : lo + LANES] = dq.astype(BF)
            dqkv_ref[r, width + lo : width + lo + LANES] = dk.astype(BF)
            dqkv_ref[r, 2 * width + lo : 2 * width + lo + LANES] = dv.astype(BF)


def block_forward(x, w_ref, d_ref, qkv_ref, probs_ref, att_ref, mid_ref, pre_ref):
    width = x.shape[1]
    u = norm(x)[0].astype(BF)
    qkv_ref[...] = mm(u, w_ref[:, : 3 * width])
    attend(qkv_ref, probs_ref, att_ref, width)
    y = x + mm(att_ref[...], w_ref[:, 3 * width : 4 * width])
    mid_ref[...] = y
    u = norm(y)[0].astype(BF)
    pre_ref[...] = mm(u, w_ref[:, 4 * width :])
    h = gelu(pre_ref[...]).astype(BF)
    return y + mm(h, d_ref[...])


def block_backward(
    g, x, w_ref, d_ref, qkv_ref, probs_ref, att_ref, mid_ref, pre_ref, dqkv_ref, put_in, put_down
):
    width = x.shape[1]
    gb = g.astype(BF)
    h, slope = gelu_both(pre_ref[...])
    put_down(h.astype(BF), gb)
    dpre = (mm_nt(gb, d_ref[...]) * slope).astype(BF)
    y = mid_ref[...]
    u, scale = norm(y)
    put_in(4 * width, u.astype(BF), dpre)
    dy = g + norm_back(u, scale, mm_nt(dpre, w_ref[:, 4 * width :]))
    gb = dy.astype(BF)
    put_in(3 * width, att_ref[...], gb)
    attend_back(
        mm_nt(gb, w_ref[:, 3 * width : 4 * width]), qkv_ref, probs_ref, dqkv_ref, width
    )
    u, scale = norm(x)
    dqkv = dqkv_ref[...]
    put_in(0, u.astype(BF), dqkv)
    return dy + norm_back(u, scale, mm_nt(dqkv, w_ref[:, : 3 * width]))


def client_forward_kernel(
    patch_ref, embed_ref, pos_ref, w_ref, d_ref,
    cut_ref, x_ref, qkv_ref, probs_ref, att_ref, mid_ref, pre_ref,
):
    rows = patch_ref.shape[0]
    x = mm(patch_ref[...], embed_ref[...])
    pos = pos_ref[...].astype(F32)
    x = x + jnp.concatenate([pos] * (rows // TOK), axis=0)
    x_ref[...] = x
    cut_ref[...] = block_forward(
        x, w_ref, d_ref, qkv_ref, probs_ref, att_ref, mid_ref, pre_ref
    ).astype(BF)


def client_backward_kernel(
    n, group,
    assign_ref, back_ref, patch_ref, w_ref, d_ref,
    x_ref, qkv_ref, probs_ref, att_ref, mid_ref, pre_ref,
    pack_ref,
    got, dqkv_ref, sem,
):
    me = lax.axis_index("client")
    shard = assign_ref[me]
    copy = pltpu.make_async_copy(back_ref.at[pl.ds(shard * group, group)], got, sem)
    copy.start()
    rows, width = x_ref.shape
    ff = d_ref.shape[0]
    r_in = w_ref.shape[1] // n
    cols = width // n
    src = lax.broadcasted_iota(jnp.int32, (width, n * PAD), 0)
    dst = lax.broadcasted_iota(jnp.int32, (width, n * PAD), 1)
    place = ((dst // PAD == src // cols) & (dst % PAD == src % cols)).astype(F32).astype(BF)
    tok = (
        lax.broadcasted_iota(jnp.int32, (rows, LANES), 0) % TOK
        == lax.broadcasted_iota(jnp.int32, (rows, LANES), 1)
    ).astype(F32).astype(BF)
    copy.wait()
    g = got[...].astype(F32).reshape(rows, width)
    per_dev = w_ref.shape[1] // n

    def put_in(start, lhs, rhs):
        for c in range(0, rhs.shape[1], width):
            part = mm_tn(rhs[:, c : c + width], lhs)
            j = (start + c) // per_dev
            pack_ref[j : j + width // per_dev, :per_dev, :] = part.reshape(
                width // per_dev, per_dev, width
            ).astype(BF)

    def put_down(h, gb):
        spread = mm(gb, place).astype(BF)
        for q in range(ff // width):
            part = mm_tn(spread, h[:, q * width : (q + 1) * width])
            lo = r_in + q * PAD
            pack_ref[:, lo : lo + PAD, :] = part.reshape(n, PAD, width).astype(BF)

    dx = block_backward(
        g, x_ref[...], w_ref, d_ref, qkv_ref, probs_ref, att_ref, mid_ref, pre_ref,
        dqkv_ref, put_in, put_down,
    )
    spread = mm(dx.astype(BF), place).astype(BF)
    lo = r_in + (ff // width) * PAD
    patch = patch_ref.shape[1]
    pack_ref[:, lo : lo + PAD, :patch] = mm_tn(spread, patch_ref[...]).reshape(
        n, PAD, patch
    ).astype(BF)
    pack_ref[:, lo : lo + PAD, width - LANES :] = mm_tn(spread, tok).reshape(
        n, PAD, LANES
    ).astype(BF)


def server_kernel(
    n, group, layers, per_image, capacity, classes, *refs,
):
    assign_ref, label_ref, arrived_ref, class_ref = refs[:4]
    refs = refs[4:]
    in_pieces, refs = refs[:group], refs[group:]
    down_pieces, refs = refs[:group], refs[group:]
    loss_ref, back_ref, gclass_ref = refs[:3]
    refs = refs[3:]
    gin_out, refs = refs[:group], refs[group:]
    gdown_out, refs = refs[:group], refs[group:]
    (
        wbuf, dbuf, gin, gdown, xs, qkv, probs, att, mid, pre, dqkv, gcur, cut,
        slot_ref, w_sem, g_sem, slot_sem,
    ) = refs
    me = lax.axis_index("client")
    rank = me % group
    shard = me // group
    rows_in = in_pieces[0].shape[1]
    rows_down = down_pieces[0].shape[1]
    piece = arrived_ref.shape[1]

    def weight_copies(layer):
        made = []
        for i in range(group):
            who = rank ^ i
            made.append(pltpu.make_async_copy(
                in_pieces[i].at[layer],
                wbuf.at[layer, pl.ds(pl.multiple_of(who * rows_in, rows_in), rows_in)],
                w_sem.at[layer, 2 * i],
            ))
            made.append(pltpu.make_async_copy(
                down_pieces[i].at[layer],
                dbuf.at[layer, pl.ds(pl.multiple_of(who * rows_down, rows_down), rows_down)],
                w_sem.at[layer, 2 * i + 1],
            ))
        return made

    def grad_copies(layer):
        made = []
        for i in range(group):
            who = rank ^ i
            made.append(pltpu.make_async_copy(
                gin.at[layer, pl.ds(pl.multiple_of(who * rows_in, rows_in), rows_in)],
                gin_out[i].at[layer],
                g_sem.at[layer, 2 * i],
            ))
            made.append(pltpu.make_async_copy(
                gdown.at[layer, pl.ds(pl.multiple_of(who * rows_down, rows_down), rows_down)],
                gdown_out[i].at[layer],
                g_sem.at[layer, 2 * i + 1],
            ))
        return made

    for layer in range(layers):
        for c in weight_copies(layer):
            c.start()

    for k in range(capacity):
        slot_ref[k] = 0

    def scan(c, count):
        hit = assign_ref[c] == shard

        @pl.when(hit)
        def _():
            slot_ref[count] = c

        return count + jnp.where(hit, 1, 0)

    filled = lax.fori_loop(0, n, scan, 0)

    def slot_in(k):
        return pltpu.make_async_copy(
            arrived_ref.at[slot_ref[k]], cut.at[pl.ds(k * piece, piece)], slot_sem.at[k]
        )

    for k in range(capacity):
        @pl.when(k < filled)
        def _():
            slot_in(k).start()

        @pl.when(k >= filled)
        def _():
            cut[k * piece : (k + 1) * piece, :] = jnp.zeros((piece, cut.shape[1]), BF)

    images = capacity * per_image
    row = lax.broadcasted_iota(jnp.int32, (images, LANES), 0)
    lane = lax.broadcasted_iota(jnp.int32, (images, LANES), 1)
    want = jnp.full((images, LANES), -1, jnp.int32)
    for k in range(capacity):
        base = slot_ref[k] * (group * per_image) + rank * per_image
        for j in range(per_image):
            lab = jnp.where(k < filled, label_ref[base + j], -1)
            want = jnp.where(row == k * per_image + j, lab, want)
    hot = (lane == want).astype(F32)
    full = (want[:, :1] >= 0).astype(F32)

    for k in range(capacity):
        @pl.when(k < filled)
        def _():
            slot_in(k).wait()

    xs[0] = cut[...].astype(F32)

    def forward(layer, carry):
        for c in weight_copies(layer):
            c.wait()
        xs[layer + 1] = block_forward(
            xs[layer], wbuf.at[layer], dbuf.at[layer], qkv.at[layer], probs.at[layer],
            att.at[layer], mid.at[layer], pre.at[layer],
        )
        return carry

    lax.fori_loop(0, layers, forward, 0)

    rows = cut.shape[0]
    pool = (
        lax.broadcasted_iota(jnp.int32, (images, rows), 1) // TOK
        == lax.broadcasted_iota(jnp.int32, (images, rows), 0)
    ).astype(F32) * (1.0 / TOK)
    unpool = (
        lax.broadcasted_iota(jnp.int32, (rows, images), 0) // TOK
        == lax.broadcasted_iota(jnp.int32, (rows, images), 1)
    ).astype(F32) * (1.0 / TOK)
    u, scale = norm(mm(pool, xs[layers], HIGH))
    pooled = u.astype(BF)
    logits = mm(pooled, class_ref[...])
    logits = jnp.where(lane < classes, logits, -1e30)
    top = jnp.max(logits, axis=-1, keepdims=True)
    e = jnp.exp(logits - top)
    total = jnp.sum(e, axis=-1, keepdims=True)
    loss = (
        jnp.log(total) + top - jnp.sum(jnp.where(lane == want, logits, 0.0), axis=-1, keepdims=True)
    ) * full
    eye = (
        lax.broadcasted_iota(jnp.int32, (images, images), 0)
        == lax.broadcasted_iota(jnp.int32, (images, images), 1)
    )
    loss_ref[...] = jnp.sum(jnp.where(eye, loss, 0.0), axis=0, keepdims=True)
    dlog = ((e / total - hot) * full).astype(BF)
    gclass_ref[...] = mm_tn(pooled, dlog).astype(BF)
    dpool = norm_back(u, scale, mm_nt(dlog, class_ref[...]))
    gcur[...] = mm(unpool, dpool, HIGH)

    def backward(i, carry):
        layer = layers - 1 - i

        def put_in(start, lhs, rhs):
            gin[layer, :, start : start + rhs.shape[1]] = mm_tn(lhs, rhs).astype(BF)

        def put_down(h, gb):
            gdown[layer] = mm_tn(h, gb).astype(BF)

        gcur[...] = block_backward(
            gcur[...], xs[layer], wbuf.at[layer], dbuf.at[layer], qkv.at[layer],
            probs.at[layer], att.at[layer], mid.at[layer], pre.at[layer], dqkv,
            put_in, put_down,
        )
        for c in grad_copies(layer):
            c.start()
        return carry

    lax.fori_loop(0, layers, backward, 0)
    cut[...] = gcur[...].astype(BF)

    def slot_out(k):
        return pltpu.make_async_copy(
            cut.at[pl.ds(k * piece, piece)], back_ref.at[slot_ref[k]], slot_sem.at[k]
        )

    for k in range(capacity):
        @pl.when(k < filled)
        def _():
            slot_out(k).start()

    for k in range(capacity):
        @pl.when(k < filled)
        def _():
            slot_out(k).wait()

    for layer in range(layers):
        for c in grad_copies(layer):
            c.wait()


def greet_all(n, me):
    barrier = pltpu.get_barrier_semaphore()

    def greet(k, carry):
        pl.semaphore_signal(
            barrier, inc=1, device_id=(lax.rem(me + k, n),), device_id_type=MESH
        )
        return carry

    lax.fori_loop(1, n, greet, 0)
    pl.semaphore_wait(barrier, n - 1)


def exchange(n, me, source, target, send_sem, recv_sem, own_sem):
    own = pltpu.make_async_copy(source(me), target.at[me], own_sem)
    own.start()

    def remote(k):
        to = lax.rem(me + k, n)
        return pltpu.make_async_remote_copy(
            src_ref=source(to), dst_ref=target.at[me], send_sem=send_sem.at[k],
            recv_sem=recv_sem.at[k], device_id=(to,), device_id_type=MESH,
        )

    def start(k, carry):
        remote(k).start()
        return carry

    def finish(k, carry):
        remote(k).wait()
        return carry

    lax.fori_loop(1, n, start, 0)
    own.wait()
    lax.fori_loop(1, n, finish, 0)


def spread_kernel(n, group, cut_ref, out_ref, send_sem, recv_sem, own_sem):
    me = lax.axis_index("client")
    greet_all(n, me)
    exchange(
        n, me, lambda to: cut_ref.at[lax.rem(to, group)], out_ref, send_sem, recv_sem, own_sem
    )


def swap_kernel(n, in_ref, out_ref, send_sem, recv_sem, own_sem):
    me = lax.axis_index("client")
    greet_all(n, me)
    exchange(n, me, lambda to: in_ref.at[to], out_ref, send_sem, recv_sem, own_sem)


def total_kernel(n, in_ref, out_ref, got, send_sem, recv_sem, own_sem):
    me = lax.axis_index("client")
    greet_all(n, me)
    exchange(n, me, lambda to: in_ref.at[to], got, send_sem, recv_sem, own_sem)
    out_ref[...] = got[0].astype(F32)

    def add(k, carry):
        out_ref[...] += got[k].astype(F32)
        return carry

    lax.fori_loop(1, n, add, 0)


def vmem():
    return pl.BlockSpec(memory_space=pltpu.VMEM)


def smem():
    return pl.BlockSpec(memory_space=pltpu.SMEM)


def hbm():
    return pl.BlockSpec(memory_space=pl.ANY)


def comm_call(kernel, out, in_spec, out_spec, scratch, n, ident, arg):
    return pl.pallas_call(
        kernel,
        out_shape=out,
        in_specs=[in_spec],
        out_specs=out_spec,
        scratch_shapes=scratch
        + [
            pltpu.SemaphoreType.DMA((n,)),
            pltpu.SemaphoreType.DMA((n,)),
            pltpu.SemaphoreType.DMA,
        ],
        compiler_params=pltpu.CompilerParams(
            collective_id=ident, has_side_effects=True, vmem_limit_bytes=VMEM_LIMIT
        ),
    )(arg)


def shape(dims, kind):
    return jax.ShapeDtypeStruct(dims, kind)


def flip(block, bit):
    n = lax.axis_size("client")
    return lax.ppermute(block, "client", [(i, i ^ (1 << bit)) for i in range(n)])


def per_device(
    patches, labels, assign, patch_embed, positions, client_in, client_down,
    server_in, server_down, classifier,
):
    n = lax.axis_size("client")
    group = n // SHARDS
    bits = group.bit_length() - 1
    me = lax.axis_index("client")
    rank = me % group
    shard = me // group
    rows = patches.shape[0]
    width = client_in.shape[0]
    cols = client_in.shape[1]
    ff = client_down.shape[0]
    layers = server_in.shape[0]
    rows_in = server_in.shape[1]
    rows_down = server_down.shape[1]
    classes = classifier.shape[2]
    piece = rows // group
    per_image = IMG // group
    capacity = SLOTS * group
    s_rows = capacity * piece
    routes = assign.reshape(n)
    params = pltpu.CompilerParams(vmem_limit_bytes=VMEM_LIMIT)

    in_pieces = [server_in]
    down_pieces = [server_down]
    for bit in range(bits):
        in_pieces = in_pieces + [flip(p, bit) for p in in_pieces]
        down_pieces = down_pieces + [flip(p, bit) for p in down_pieces]

    def kept(r):
        return [
            shape((r, 3 * width), F32),
            shape((r // LANES * HEADS, LANES, LANES), BF),
            shape((r, width), BF),
            shape((r, width), F32),
            shape((r, ff), F32),
        ]

    cut, x0, *saved = pl.pallas_call(
        client_forward_kernel,
        out_shape=[shape((rows, width), BF), shape((rows, width), F32)] + kept(rows),
        in_specs=[vmem()] * 5,
        out_specs=[vmem()] * 7,
        compiler_params=params,
    )(patches, patch_embed, positions, client_in, client_down)

    arrived = comm_call(
        functools.partial(spread_kernel, n, group),
        shape((n, piece, width), BF), vmem(), hbm(), [], n, 1,
        cut.reshape(group, piece, width),
    )

    class_shard = jnp.pad(
        lax.dynamic_index_in_dim(classifier, shard, 0, keepdims=False),
        ((0, 0), (0, LANES - classes)),
    )
    part_in = shape((layers, rows_in, cols), BF)
    part_down = shape((layers, rows_down, width), BF)
    res = pl.pallas_call(
        functools.partial(server_kernel, n, group, layers, per_image, capacity, classes),
        out_shape=[
            shape((1, capacity * per_image), F32),
            shape((n, piece, width), BF),
            shape((width, LANES), BF),
        ]
        + [part_in] * group
        + [part_down] * group,
        in_specs=[smem(), smem(), hbm(), vmem()] + [hbm()] * (2 * group),
        out_specs=[vmem(), hbm(), vmem()] + [hbm()] * (2 * group),
        scratch_shapes=[
            pltpu.VMEM((layers, width, cols), BF),
            pltpu.VMEM((layers, ff, width), BF),
            pltpu.VMEM((layers, width, cols), BF),
            pltpu.VMEM((layers, ff, width), BF),
            pltpu.VMEM((layers + 1, s_rows, width), F32),
        ]
        + [pltpu.VMEM((layers,) + s.shape, s.dtype) for s in kept(s_rows)]
        + [
            pltpu.VMEM((s_rows, 3 * width), BF),
            pltpu.VMEM((s_rows, width), F32),
            pltpu.VMEM((s_rows, width), BF),
            pltpu.SMEM((capacity,), jnp.int32),
            pltpu.SemaphoreType.DMA((layers, 2 * group)),
            pltpu.SemaphoreType.DMA((layers, 2 * group)),
            pltpu.SemaphoreType.DMA((capacity,)),
        ],
        compiler_params=params,
    )(routes, labels, arrived, class_shard, *in_pieces, *down_pieces)
    losses, back, gclass = res[:3]
    parts_in = list(res[3 : 3 + group])
    parts_down = list(res[3 + group :])

    returned = comm_call(
        functools.partial(swap_kernel, n),
        shape((n, piece, width), BF), hbm(), hbm(), [], n, 2, back,
    )

    half = group // 2
    while half:
        bit = half.bit_length() - 1
        parts_in = [
            parts_in[i].astype(F32) + flip(parts_in[i + half].astype(BF), bit).astype(F32)
            for i in range(half)
        ]
        parts_down = [
            parts_down[i].astype(F32) + flip(parts_down[i + half].astype(BF), bit).astype(F32)
            for i in range(half)
        ]
        half //= 2
    gsum = gclass.astype(F32)
    for bit in range(bits):
        gsum = gsum + flip(gsum.astype(BF), bit).astype(F32)
    grad_class = lax.dynamic_slice_in_dim(gsum, rank * rows_in, rows_in, 0)[:, :classes]

    r_in = cols // n
    pack_rows = r_in + (ff // width + 1) * PAD
    packed = pl.pallas_call(
        functools.partial(client_backward_kernel, n, group),
        out_shape=shape((n, pack_rows, width), BF),
        in_specs=[smem(), hbm()] + [vmem()] * 9,
        out_specs=vmem(),
        scratch_shapes=[
            pltpu.VMEM((group, piece, width), BF),
            pltpu.VMEM((rows, 3 * width), BF),
            pltpu.SemaphoreType.DMA,
        ],
        compiler_params=params,
    )(routes, returned, patches, client_in, client_down, x0, *saved)

    summed = comm_call(
        functools.partial(total_kernel, n),
        shape((pack_rows, width), F32), vmem(), vmem(),
        [pltpu.VMEM((n, pack_rows, width), BF)], n, 3, packed,
    )
    own = width // n
    tail = summed[r_in:].reshape(ff // width + 1, PAD, width)[:, :own]
    grad_in = summed[:r_in].T
    grad_down = tail[:-1].transpose(0, 2, 1).reshape(ff, own)
    last = tail[-1].T
    patch = patches.shape[1]
    return (
        losses,
        last[:patch],
        last[width - LANES : width - LANES + TOK],
        grad_in,
        grad_down,
        parts_in[0],
        parts_down[0],
        grad_class,
    )


def solution(mesh):
    whole = P()
    in_specs = (
        P("client", None), whole, whole, whole, whole, whole, whole,
        P(None, "client", None), P(None, "client", None), whole,
    )
    out_specs = (
        P("client", None), P(None, "client"), P(None, "client"), P(None, "client"),
        P(None, "client"), P(None, "client", None), P(None, "client", None), P("client", None),
    )
    return jax.shard_map(
        per_device, mesh=mesh, in_specs=in_specs, out_specs=out_specs, check_vma=False
    )
```

profile of v0, /device:TPU:15, one launch (start us, length us, event | category | flops | bytes accessed | tf_op | source)
XLA Modules:
  0.0 266.5 jit_solution(24021626788644600)
XLA Ops:
  0.6 0.0 copy-start
  0.6 0.7 collective-permute-start
  1.4 0.1 collective-permute-start.1
  1.5 1.5 copy.18.patch_ref
  3.0 0.0 copy-done
  3.0 0.1 copy.19
  3.2 6.0 %shard_map.161 = (bf16[128,384]{1,0:T(8,128)(2,1)}, f32[128,384]{1,0:T(8,128)}, f32[128,1152]{1,0:T(8,128)}, bf16[6,128,128]{2,1,0:T(8,128)(2,1)}, bf16[128,384]...) custom-call(bf16[128,192]{1,0:T(8,128)(2,1)} %copy.18.patch_ref, bf16[192,384]{1,0:T(8,128)(2,1)} %embed_ref.1, ...), custom_call_target="tpu_custom_call" | custom-call | tf_op jit(solution)/shard_map/pallas_call | solution.py:571
  9.2 43.1 %shard_map.162.refs_2_ = bf16[32,64,384]{2,1,0:T(8,128)(2,1)} custom-call(bf16[2,64,384]{2,1,0:T(8,128)(2,1)} %bitcast.25), custom_call_target="tpu_custom_call" | custom-call | tf_op jit(solution)/shard_map/pallas_call | solution.py:505
  52.3 0.7 pad.4.refs_3_
  52.9 0.0 collective-permute-done.1.refs_7_
  52.9 0.0 collective-permute-done.refs_5_
  52.9 0.0 copy-start.1
  52.9 1.4 copy-done.1
  54.3 30.3 %shard_map.163 = (f32[1,16]{1,0:T(1,128)}, bf16[32,64,384]{2,1,0:T(8,128)(2,1)}, bf16[384,128]{1,0:T(8,128)(2,1)}, bf16[2,192,3072]{2,1,0:T(8,128)(2,1)}, bf16[2...) custom-call(s32[32]{0:T(128)} %bitcast.27, s32[256]{0:T(256)} %refs_1_.1, ...), custom_call_target="tpu_custom_call" | custom-call | tf_op jit(solution)/shard_map/pallas_call | solution.py:591
  84.6 0.1 collective-permute-start.2
  84.7 0.5 collective-permute-start.3
  85.2 0.1 collective-permute-start.4
  85.3 40.6 %shard_map.164.back_ref = bf16[32,64,384]{2,1,0:T(8,128)(2,1)} custom-call(bf16[32,64,384]{2,1,0:T(8,128)(2,1)} %get-tuple-element.24.in_ref), custom_call_target="tpu_custom_call" | custom-call | tf_op jit(solution)/shard_map/pallas_call | solution.py:505
  125.9 10.2 %shard_map.165.in_ref = bf16[32,176,384]{2,1,0:T(8,128)(2,1)} custom-call(s32[32]{0:T(128)} %bitcast.28, bf16[32,64,384]{2,1,0:T(8,128)(2,1)} %shard_map.164.back_ref, bf16[128,192]{1,0:T(8,128)(2,1)} %copy.18.patch_ref, bf16[384,3072]{1,0:T(8,128)(2,1)} %w_ref.3, bf16[1536,384]{1,0:T(8,128)(2,1)} %d_ref.3, f32[128,384]{1,0:T(8,128)} %get-tuple-element.25.x_ref, ...), custom_call_target="tpu_custom_call" | custom-call | tf_op jit(solution)/shard_map/pallas_call | solution.py:649
  136.1 0.0 copy-start.3
  136.1 118.5 %shard_map.166 = f32[176,384]{1,0:T(8,128)} custom-call(bf16[32,176,384]{2,1,0:T(8,128)(2,1)} %shard_map.165.in_ref), custom_call_target="tpu_custom_call" | custom-call | tf_op jit(solution)/shard_map/pallas_call | solution.py:505
  254.6 0.9 slice.24
  255.5 1.6 slice_bitcast_fusion
  257.1 0.1 copy.25
  257.3 0.6 slice.33
  258.0 0.6 copy.26
  258.6 0.7 copy.23
  259.3 0.0 collective-permute-done.4
  259.3 0.0 copy-done.3
  259.3 0.7 copy.24
  260.0 0.0 collective-permute-done.3
  260.0 0.0 copy-start.2
  260.0 3.4 %convert_add_fusion.1 = f32[2,768,384]{2,1,0:T(8,128)} fusion(bf16[2,768,384]{2,1,0:T(8,128)(2,1)} %collective-permute-done.3, bf16[2,768,384]{2,1,0:T(8,128)(2,1)} %get-tuple-element.33), kind=kLoop, calls=%fused_computation.1 | loop fusion | flops 1769472 | bytes 4718592 | tf_op jit(solution)/shard_map/add | solution.py:638
  263.4 0.0 collective-permute-done.2
  263.4 0.0 copy-done.2
  263.4 3.0 %convert_add_fusion = f32[2,192,3072]{2,1,0:T(8,128)} fusion(bf16[2,192,3072]{2,1,0:T(8,128)(2,1)S(1)} %collective-permute-done.2, bf16[2,192,3072]{2,1,0:T(8,128)(2,1)S(1)} %copy-done.2), kind=kLoop, calls=%fused_computation | loop fusion | flops 3538944 | bytes 9437184 | tf_op jit(solution)/shard_map/add | solution.py:634
  (7 shorter events, 0.1 us)
Async XLA Ops:
  0.6 2.4 copy-start
  0.6 52.3 %collective-permute-start = (bf16[2,192,3072]{2,1,0:T(8,128)(2,1)}, bf16[2,192,3072]{2,1,0:T(8,128)(2,1)S(1)}, u32[]{:S(2)}, u32[]{:S(2)}) collective-permute-start(bf16[2,192,3072]{2,1,0:T(8,128)(2,1)} %refs_4_.1), channel_id=1, source_target_pairs={{0,1},{1,0},{2,3},{3,2},{4,5},{5,4},{6,7},{7,6},{8,9},{9,8},{10,11... | collective-permute-start | bytes 7077896 | tf_op jit(solution)/shard_map/ppermute | solution.py:528
  1.4 51.5 %collective-permute-start.1 = (bf16[2,768,384]{2,1,0:T(8,128)(2,1)}, bf16[2,768,384]{2,1,0:T(8,128)(2,1)}, u32[]{:S(2)}, u32[]{:S(2)}) collective-permute-start(bf16[2,768,384]{2,1,0:T(8,128)(2,1)} %refs_6_.1), channel_id=1, source_target_pairs={{0,1},{1,0},{2,3},{3,2},{4,5},{5,4},{6,7},{7,6},{8,9},{9,8},{10,11... | collective-permute-start | bytes 3538952 | tf_op jit(solution)/shard_map/ppermute | solution.py:528
  52.9 1.4 copy-start.1
  84.6 178.8 %collective-permute-start.2 = (bf16[2,192,3072]{2,1,0:T(8,128)(2,1)}, bf16[2,192,3072]{2,1,0:T(8,128)(2,1)S(1)}, u32[]{:S(2)}, u32[]{:S(2)}) collective-permute-start(bf16[2,192,3072]{2,1,0:T(8,128)(2,1)} %get-tuple-element.32), channel_id=1, source_target_pairs={{0,1},{1,0},{2,3},{3,2},{4,5},{5,4},{6,7},{7,6},{8,9},{9,8},{10,11... | collective-permute-start | bytes 7077896 | tf_op jit(solution)/shard_map/ppermute | solution.py:528
  84.7 175.3 %collective-permute-start.3 = (bf16[2,768,384]{2,1,0:T(8,128)(2,1)}, bf16[2,768,384]{2,1,0:T(8,128)(2,1)}, u32[]{:S(2)}, u32[]{:S(2)}) collective-permute-start(bf16[2,768,384]{2,1,0:T(8,128)(2,1)} %get-tuple-element.34), channel_id=1, source_target_pairs={{0,1},{1,0},{2,3},{3,2},{4,5},{5,4},{6,7},{7,6},{8,9},{9,8},{10,11... | collective-permute-start | bytes 3538952 | tf_op jit(solution)/shard_map/ppermute | solution.py:528
  85.2 174.1 %collective-permute-start.4 = (bf16[384,128]{1,0:T(8,128)(2,1)}, bf16[384,128]{1,0:T(8,128)(2,1)S(1)}, u32[]{:S(2)}, u32[]{:S(2)}) collective-permute-start(bf16[384,128]{1,0:T(8,128)(2,1)} %get-tuple-element.35), channel_id=1, source_target_pairs={{0,1},{1,0},{2,3},{3,2},{4,5},{5,4},{6,7},{7,6},{8,9},{9,8},{10,11... | collective-permute-start | bytes 294920 | tf_op jit(solution)/shard_map/ppermute | solution.py:528
  136.1 123.2 %copy-start.3 = (bf16[384,128]{1,0:T(8,128)(2,1)S(1)}, bf16[384,128]{1,0:T(8,128)(2,1)}, u32[]{:S(2)}) copy-start(bf16[384,128]{1,0:T(8,128)(2,1)} %get-tuple-element.35) | copy-start | bytes 294916
  260.0 3.4 %copy-start.2 = (bf16[2,192,3072]{2,1,0:T(8,128)(2,1)S(1)}, bf16[2,192,3072]{2,1,0:T(8,128)(2,1)}, u32[]{:S(2)}) copy-start(bf16[2,192,3072]{2,1,0:T(8,128)(2,1)} %get-tuple-element.31) | copy-start | bytes 7077892
where the time goes:
time: 266 us
  Pallas kernels  249 us (94%)
  local copies, waits for them, and re-layouts  9.11 us (3%)
  other arithmetic  6.46 us (2%)
    pallas_call x3, Pallas kernels, comm_call(): pl.pallas_call(kernel, out_shape=out, in_specs=[in_spec], out_specs=out_s...  202 us
    pallas_call x1, Pallas kernels, per_device(): pl.pallas_call(functools.partial(server_kernel, n, group, layers, per_ima...  30.3 us
    pallas_call x1, Pallas kernels, per_device(): pl.pallas_call(functools.partial(client_backward_kernel, n, group), out_s...  10.2 us
    pallas_call x1, Pallas kernels, per_device(): pl.pallas_call(client_forward_kernel, out_shape=[shape((rows, width), BF)...  5.96 us
  transfers between devices with their start and end apart: 5, of which 0 were waited for; matrix products, arithmetic and copies ran while one was open for 4% of the time, Pallas kernels for 82%

commit v1 on v0

v1 whole, which is shorter than its diff:
```python
import functools
import math

import jax
import jax.numpy as jnp
from jax import lax
from jax.experimental import pallas as pl
from jax.experimental.pallas import tpu as pltpu
from jax.sharding import PartitionSpec as P

HEADS = 6
TOK = 16
IMG = 8
SHARDS = 16
SLOTS = 2
PLANE = 4
EPSILON = 1e-06
LANES = 128
PAD = 16
BF = jnp.bfloat16
F32 = jnp.float32
HIGH = lax.Precision.HIGHEST
GELU_C = math.sqrt(2.0 / math.pi)
VMEM_LIMIT = 60 * 1024 * 1024
MESH = pl.DeviceIdType.MESH


def mm(a, b, precision=None):
    return lax.dot_general(
        a, b, (((1,), (0,)), ((), ())), precision=precision, preferred_element_type=F32
    )


def mm_nt(a, b, precision=None):
    return lax.dot_general(
        a, b, (((1,), (1,)), ((), ())), precision=precision, preferred_element_type=F32
    )


def mm_tn(a, b):
    return lax.dot_general(a, b, (((0,), (0,)), ((), ())), preferred_element_type=F32)


def norm(v):
    centre = v - jnp.mean(v, axis=-1, keepdims=True)
    scale = lax.rsqrt(jnp.mean(centre * centre, axis=-1, keepdims=True) + EPSILON)
    return centre * scale, scale


def norm_back(normed, scale, grad):
    return scale * (
        grad
        - jnp.mean(grad, axis=-1, keepdims=True)
        - normed * jnp.mean(grad * normed, axis=-1, keepdims=True)
    )


def gelu(v):
    t = jnp.tanh(GELU_C * (v + 0.044715 * (v * v * v)))
    return 0.5 * v * (1.0 + t)


def gelu_both(v):
    sq = v * v
    t = jnp.tanh(GELU_C * (v + 0.044715 * (sq * v)))
    value = 0.5 * v * (1.0 + t)
    slope = 0.5 * (1.0 + t) + 0.5 * v * (1.0 - t * t) * (GELU_C * (1.0 + 0.134145 * sq))
    return value, slope


def image_mask():
    row = lax.broadcasted_iota(jnp.int32, (LANES, LANES), 0)
    col = lax.broadcasted_iota(jnp.int32, (LANES, LANES), 1)
    return row // TOK == col // TOK


def lane_masks(head_dim):
    lane = lax.broadcasted_iota(jnp.int32, (LANES, LANES), 1)
    return [lane // head_dim == h for h in range(LANES // head_dim)]


def attend(qkv_ref, probs_ref, att_ref, width):
    rows = qkv_ref.shape[0]
    head_dim = width // HEADS
    per = LANES // head_dim
    inside = image_mask()
    keeps = lane_masks(head_dim)
    for group in range(rows // LANES):
        r = slice(group * LANES, (group + 1) * LANES)
        for pair in range(width // LANES):
            lo = pair * LANES
            q = qkv_ref[r, lo : lo + LANES]
            k = qkv_ref[r, width + lo : width + lo + LANES]
            v = qkv_ref[r, 2 * width + lo : 2 * width + lo + LANES]
            out = jnp.zeros((LANES, LANES), F32)
            for h in range(per):
                s = mm_nt(jnp.where(keeps[h], q, 0.0), k, HIGH) * (1.0 / math.sqrt(head_dim))
                s = jnp.where(inside, s, -1e30)
                e = jnp.exp(s - jnp.max(s, axis=-1, keepdims=True))
                p = (e / jnp.sum(e, axis=-1, keepdims=True)).astype(BF)
                probs_ref[group * HEADS + pair * per + h] = p
                out = out + mm(p, jnp.where(keeps[h], v, 0.0).astype(BF))
            att_ref[r, lo : lo + LANES] = out.astype(BF)


def attend_back(grad, qkv_ref, probs_ref, dqkv_ref, width):
    rows = qkv_ref.shape[0]
    head_dim = width // HEADS
    per = LANES // head_dim
    keeps = lane_masks(head_dim)
    for group in range(rows // LANES):
        r = slice(group * LANES, (group + 1) * LANES)
        for pair in range(width // LANES):
            lo = pair * LANES
            q = qkv_ref[r, lo : lo + LANES]
            k = qkv_ref[r, width + lo : width + lo + LANES]
            v = qkv_ref[r, 2 * width + lo : 2 * width + lo + LANES].astype(BF)
            go = grad[r, lo : lo + LANES]
            dq = jnp.zeros((LANES, LANES), F32)
            dk = jnp.zeros((LANES, LANES), F32)
            dv = jnp.zeros((LANES, LANES), F32)
            for h in range(per):
                p = probs_ref[group * HEADS + pair * per + h]
                goh = jnp.where(keeps[h], go, 0.0).astype(BF)
                dp = mm_nt(goh, v)
                dv = dv + mm_tn(p, goh)
                pf = p.astype(F32)
                ds = pf * (dp - jnp.sum(pf * dp, axis=-1, keepdims=True))
                ds = (ds * (1.0 / math.sqrt(head_dim))).astype(BF)
                dq = dq + mm(ds, jnp.where(keeps[h], k, 0.0).astype(BF))
                dk = dk + mm_tn(ds, jnp.where(keeps[h], q, 0.0).astype(BF))
            dqkv_ref[r, lo : lo + LANES] = dq.astype(BF)
            dqkv_ref[r, width + lo : width + lo + LANES] = dk.astype(BF)
            dqkv_ref[r, 2 * width + lo : 2 * width + lo + LANES] = dv.astype(BF)


def block_forward(x, w_ref, d_ref, qkv_ref, probs_ref, att_ref, mid_ref, pre_ref):
    width = x.shape[1]
    u = norm(x)[0].astype(BF)
    qkv_ref[...] = mm(u, w_ref[:, : 3 * width])
    attend(qkv_ref, probs_ref, att_ref, width)
    y = x + mm(att_ref[...], w_ref[:, 3 * width : 4 * width])
    mid_ref[...] = y
    u = norm(y)[0].astype(BF)
    pre_ref[...] = mm(u, w_ref[:, 4 * width :])
    h = gelu(pre_ref[...]).astype(BF)
    return y + mm(h, d_ref[...])


def block_backward(
    g, x, w_ref, d_ref, qkv_ref, probs_ref, att_ref, mid_ref, pre_ref, dqkv_ref, put_in, put_down
):
    width = x.shape[1]
    gb = g.astype(BF)
    h, slope = gelu_both(pre_ref[...])
    put_down(h.astype(BF), gb)
    dpre = (mm_nt(gb, d_ref[...]) * slope).astype(BF)
    y = mid_ref[...]
    u, scale = norm(y)
    put_in(4 * width, u.astype(BF), dpre)
    dy = g + norm_back(u, scale, mm_nt(dpre, w_ref[:, 4 * width :]))
    gb = dy.astype(BF)
    put_in(3 * width, att_ref[...], gb)
    attend_back(
        mm_nt(gb, w_ref[:, 3 * width : 4 * width]), qkv_ref, probs_ref, dqkv_ref, width
    )
    u, scale = norm(x)
    dqkv = dqkv_ref[...]
    put_in(0, u.astype(BF), dqkv)
    return dy + norm_back(u, scale, mm_nt(dqkv, w_ref[:, : 3 * width]))


def bits_of(n):
    return n.bit_length() - 1


def part_orders(n):
    rest = list(range(1, bits_of(n)))
    far = rest[-2:]
    near = rest[:-2]
    low = near[: len(near) // 2]
    high = near[len(near) // 2 :]
    return [[0] + low + high + far, [0] + high + low + far, [0] + far + low + high]


def place_of(device, order):
    index = 0
    for bit in order:
        index = index * 2 + (device >> bit & 1)
    return index


def split_rows(r_in):
    return r_in - PAD if r_in >= 4 * PAD else r_in


def gather_kernel(
    n, group, capacity,
    assign_ref, patch_ref,
    slots_ref, table_ref,
    column, pack, got, near_send, near_recv, far_send, far_recv, flat_send, flat_recv,
):
    me = lax.axis_index("client")
    rank = me % group
    shard = me // group
    line = shard // PLANE
    spot = shard % PLANE
    barrier = pltpu.get_barrier_semaphore()

    def near_peer(i):
        return shard * group + lax.rem(rank + i, group)

    def far_peer(i):
        return (lax.rem(line + i, PLANE) * PLANE + spot) * group + rank

    def flat_peer(i):
        return (line * PLANE + lax.rem(spot + i, PLANE)) * group + rank

    peers = [near_peer(i) for i in range(1, group)]
    peers += [far_peer(i) for i in range(1, PLANE)]
    peers += [flat_peer(i) for i in range(1, PLANE)]
    for peer in peers:
        pl.semaphore_signal(barrier, inc=1, device_id=(peer,), device_id_type=MESH)
    pl.semaphore_wait(barrier, len(peers))

    def near(i):
        to = lax.rem(rank + i, group)
        return pltpu.make_async_remote_copy(
            src_ref=patch_ref.at[to], dst_ref=column.at[line, rank], send_sem=near_send.at[i],
            recv_sem=near_recv.at[i], device_id=(near_peer(i),), device_id_type=MESH,
        )

    def far(i, j):
        if j == 0:
            source, member = patch_ref.at[rank], rank
        else:
            member = lax.rem(rank + group - j, group)
            source = column.at[line, member]
        return pltpu.make_async_remote_copy(
            src_ref=source, dst_ref=column.at[line, member], send_sem=far_send.at[i, j],
            recv_sem=far_recv.at[i, j], device_id=(far_peer(i),), device_id_type=MESH,
        )

    def flat(i):
        return pltpu.make_async_remote_copy(
            src_ref=pack.at[i], dst_ref=got.at[spot], send_sem=flat_send.at[i],
            recv_sem=flat_recv.at[i], device_id=(flat_peer(i),), device_id_type=MESH,
        )

    for i in range(1, group):
        near(i).start()
    for i in range(1, PLANE):
        far(i, 0).start()
    for j in range(1, group):
        near(j).wait_recv()
        for i in range(1, PLANE):
            far(i, j).start()
    column[line, rank] = patch_ref[rank]

    targets = [line * PLANE + lax.rem(spot + i, PLANE) for i in range(PLANE)]

    def scan(c, carry):
        there = assign_ref[c]
        out = []
        for i in range(PLANE):
            count, slots = carry[i]
            hit = there == targets[i]
            slots = tuple(
                jnp.where(hit & (count == k), c, slots[k]) for k in range(capacity)
            )
            out.append((count + jnp.where(hit, 1, 0), slots))
        return tuple(out)

    zero = jnp.int32(0)
    table = lax.fori_loop(
        0, n, scan, tuple((zero, tuple(zero for _ in range(capacity))) for _ in range(PLANE))
    )
    for i in range(1, PLANE):
        for j in range(group):
            far(i, j).wait_recv()

    def pick(c):
        home = c // group
        return column[home // PLANE, c % group]

    for i in range(1, PLANE):
        for k in range(capacity):
            pack[i, k] = pick(table[i][1][k])
    for i in range(1, PLANE):
        flat(i).start()
    count, slots = table[0]
    for k in range(capacity):
        got[spot, k] = pick(slots[k])
        table_ref[k] = slots[k]
    table_ref[capacity] = count
    for i in range(1, PLANE):
        flat(i).wait_recv()
    piece = patch_ref.shape[1]
    for k in range(capacity):
        home = slots[k] // group
        slots_ref[k * piece : (k + 1) * piece, :] = got[home % PLANE, k]
    for i in range(1, group):
        near(i).wait_send()
    for i in range(1, PLANE):
        for j in range(group):
            far(i, j).wait_send()
        flat(i).wait_send()


def step_kernel(
    n, group, layers, per_image, capacity, classes, *refs,
):
    table_ref, label_ref, patch_ref, embed_ref, pos_ref, class_ref, cin_ref, cdown_ref = refs[:8]
    refs = refs[8:]
    in_pieces, refs = refs[:group], refs[group:]
    down_pieces, refs = refs[:group], refs[group:]
    loss_ref, gclass_ref, pack_a, pack_b, pack_c = refs[:5]
    refs = refs[5:]
    gin_out, refs = refs[:group], refs[group:]
    gdown_out, refs = refs[:group], refs[group:]
    (
        wbuf, dbuf, gin, gdown, xs, qkv, probs, att, mid, pre, dqkv, gcur, cls,
        w_sem, g_sem, c_sem,
    ) = refs
    me = lax.axis_index("client")
    rank = me % group
    shard = me // group
    rows_in = in_pieces[0].shape[1]
    rows_down = down_pieces[0].shape[1]
    rows, width = gcur.shape
    ff = dbuf.shape[1]

    def client_copies():
        return [
            pltpu.make_async_copy(cin_ref, wbuf.at[0], c_sem.at[0]),
            pltpu.make_async_copy(cdown_ref, dbuf.at[0], c_sem.at[1]),
        ]

    def class_copy():
        return pltpu.make_async_copy(class_ref.at[shard], cls, c_sem.at[2])

    def weight_copies(layer):
        made = []
        for i in range(group):
            who = rank ^ i
            made.append(pltpu.make_async_copy(
                in_pieces[i].at[layer],
                wbuf.at[layer + 1, pl.ds(pl.multiple_of(who * rows_in, rows_in), rows_in)],
                w_sem.at[layer, 2 * i],
            ))
            made.append(pltpu.make_async_copy(
                down_pieces[i].at[layer],
                dbuf.at[layer + 1, pl.ds(pl.multiple_of(who * rows_down, rows_down), rows_down)],
                w_sem.at[layer, 2 * i + 1],
            ))
        return made

    def grad_copies(layer):
        made = []
        for i in range(group):
            who = rank ^ i
            made.append(pltpu.make_async_copy(
                gin.at[layer, pl.ds(pl.multiple_of(who * rows_in, rows_in), rows_in)],
                gin_out[i].at[layer],
                g_sem.at[layer, 2 * i],
            ))
            made.append(pltpu.make_async_copy(
                gdown.at[layer, pl.ds(pl.multiple_of(who * rows_down, rows_down), rows_down)],
                gdown_out[i].at[layer],
                g_sem.at[layer, 2 * i + 1],
            ))
        return made

    for c in client_copies():
        c.start()
    class_copy().start()
    for layer in range(layers):
        for c in weight_copies(layer):
            c.start()

    images = capacity * per_image
    row = lax.broadcasted_iota(jnp.int32, (images, classes), 0)
    lane = lax.broadcasted_iota(jnp.int32, (images, classes), 1)
    want = jnp.full((images, classes), -1, jnp.int32)
    filled = table_ref[capacity]
    for k in range(capacity):
        base = table_ref[k] * (group * per_image) + rank * per_image
        for j in range(per_image):
            lab = jnp.where(k < filled, label_ref[base + j], -1)
            want = jnp.where(row == k * per_image + j, lab, want)
    hot = (lane == want).astype(F32)
    full = (want[:, :1] >= 0).astype(F32)

    x = mm(patch_ref[...], embed_ref[...])
    pos = pos_ref[...].astype(F32)
    xs[0] = x + jnp.concatenate([pos] * (rows // TOK), axis=0)
    for c in client_copies():
        c.wait()

    def forward(layer, carry):
        @pl.when(layer > 0)
        def _():
            for c in weight_copies(layer - 1):
                c.wait()

        out = block_forward(
            xs[layer], wbuf.at[layer], dbuf.at[layer], qkv.at[layer], probs.at[layer],
            att.at[layer], mid.at[layer], pre.at[layer],
        )
        xs[layer + 1] = jnp.where(layer == 0, out.astype(BF).astype(F32), out)
        return carry

    lax.fori_loop(0, layers + 1, forward, 0)

    pool = (
        lax.broadcasted_iota(jnp.int32, (images, rows), 1) // TOK
        == lax.broadcasted_iota(jnp.int32, (images, rows), 0)
    ).astype(F32) * (1.0 / TOK)
    unpool = (
        lax.broadcasted_iota(jnp.int32, (rows, images), 0) // TOK
        == lax.broadcasted_iota(jnp.int32, (rows, images), 1)
    ).astype(F32) * (1.0 / TOK)
    class_copy().wait()
    u, scale = norm(mm(pool, xs[layers + 1], HIGH))
    pooled = u.astype(BF)
    logits = mm(pooled, cls[...])
    top = jnp.max(logits, axis=-1, keepdims=True)
    e = jnp.exp(logits - top)
    total = jnp.sum(e, axis=-1, keepdims=True)
    loss = (
        jnp.log(total) + top - jnp.sum(jnp.where(lane == want, logits, 0.0), axis=-1, keepdims=True)
    ) * full
    eye = (
        lax.broadcasted_iota(jnp.int32, (images, images), 0)
        == lax.broadcasted_iota(jnp.int32, (images, images), 1)
    )
    loss_ref[...] = jnp.sum(jnp.where(eye, loss, 0.0), axis=0, keepdims=True)
    dlog = ((e / total - hot) * full).astype(BF)
    gclass_ref[...] = mm_tn(pooled, dlog).astype(BF)
    dpool = norm_back(u, scale, mm_nt(dlog, cls[...]))
    gcur[...] = mm(unpool, dpool, HIGH)

    def backward(i, carry):
        layer = layers - 1 - i

        def put_in(start, lhs, rhs):
            gin[layer, :, start : start + rhs.shape[1]] = mm_tn(lhs, rhs).astype(BF)

        def put_down(h, gb):
            gdown[layer] = mm_tn(h, gb).astype(BF)

        deep = layer + 1
        gcur[...] = block_backward(
            gcur[...], xs[deep], wbuf.at[deep], dbuf.at[deep], qkv.at[deep],
            probs.at[deep], att.at[deep], mid.at[deep], pre.at[deep], dqkv,
            put_in, put_down,
        )
        for c in grad_copies(layer):
            c.start()
        return carry

    lax.fori_loop(0, layers, backward, 0)

    orders = part_orders(n)
    per_dev = wbuf.shape[2] // n
    head = split_rows(per_dev)
    cols = width // n
    src = lax.broadcasted_iota(jnp.int32, (width, n * PAD), 0)
    dst = lax.broadcasted_iota(jnp.int32, (width, n * PAD), 1)
    spread_to = ((dst // PAD == src // cols) & (dst % PAD == src % cols)).astype(F32).astype(BF)
    tok = (
        lax.broadcasted_iota(jnp.int32, (rows, LANES), 0) % TOK
        == lax.broadcasted_iota(jnp.int32, (rows, LANES), 1)
    ).astype(F32).astype(BF)

    def put_in(start, lhs, rhs):
        for c in range(0, rhs.shape[1], width):
            part = mm_tn(rhs[:, c : c + width], lhs).astype(BF)
            first = (start + c) // per_dev
            for j in range(width // per_dev):
                lo = j * per_dev
                pack_a[place_of(first + j, orders[0])] = part[lo : lo + head]
                if head < per_dev:
                    pack_b[place_of(first + j, orders[1]), : per_dev - head] = (
                        part[lo + head : lo + per_dev]
                    )

    def put_down(h, gb):
        spread = mm(gb, spread_to).astype(BF)
        last = ff // width - 1
        for q in range(ff // width):
            part = mm_tn(spread, h[:, q * width : (q + 1) * width]).astype(BF)
            lo = per_dev - head + q * PAD
            for j in range(n):
                value = part[j * PAD : (j + 1) * PAD]
                if q == last:
                    pack_c[place_of(j, orders[2]), :PAD] = value
                else:
                    pack_b[place_of(j, orders[1]), lo : lo + PAD] = value

    dx = block_backward(
        gcur[...].astype(BF).astype(F32), xs[0], wbuf.at[0], dbuf.at[0], qkv.at[0],
        probs.at[0], att.at[0], mid.at[0], pre.at[0], dqkv, put_in, put_down,
    )
    spread = mm(dx.astype(BF), spread_to).astype(BF)
    patch = patch_ref.shape[1]
    embed_part = mm_tn(spread, patch_ref[...]).astype(BF)
    pos_part = mm_tn(spread, tok).astype(BF)
    for j in range(n):
        at = place_of(j, orders[2])
        pack_c[at, PAD : 2 * PAD, :patch] = embed_part[j * PAD : (j + 1) * PAD]
        pack_c[at, PAD : 2 * PAD, patch : width - LANES] = jnp.zeros(
            (PAD, width - LANES - patch), BF
        )
        pack_c[at, PAD : 2 * PAD, width - LANES :] = pos_part[j * PAD : (j + 1) * PAD]

    for layer in range(layers):
        for c in grad_copies(layer):
            c.wait()


def reduce_kernel(n, *refs):
    steps = bits_of(n)
    orders = part_orders(n)
    parts = len(orders)
    packs, refs = refs[:parts], refs[parts:]
    outs, refs = refs[:parts], refs[parts:]
    got = [refs[q * steps : (q + 1) * steps] for q in range(parts)]
    refs = refs[parts * steps :]
    held = [refs[q * (steps - 1) : (q + 1) * (steps - 1)] for q in range(parts)]
    send_sem, recv_sem = refs[parts * (steps - 1) :]
    me = lax.axis_index("client")
    barrier = pltpu.get_barrier_semaphore()

    def peer(bit):
        return me + (1 << bit) - 2 * (1 << bit) * (me // (1 << bit) % 2)

    for bit in range(steps):
        pl.semaphore_signal(barrier, inc=1, device_id=(peer(bit),), device_id_type=MESH)
    pl.semaphore_wait(barrier, steps)

    def source(q, t):
        return packs[q] if t == 0 else held[q][t - 1]

    def mine(q, t):
        return me // (1 << orders[q][t]) % 2

    def copy(q, t):
        half = n >> (t + 1)
        return pltpu.make_async_remote_copy(
            src_ref=source(q, t).at[pl.ds((1 - mine(q, t)) * half, half)], dst_ref=got[q][t],
            send_sem=send_sem.at[q, t], recv_sem=recv_sem.at[q, t],
            device_id=(peer(orders[q][t]),), device_id_type=MESH,
        )

    for q in range(parts):
        copy(q, 0).start()
    for t in range(steps):
        half = n >> (t + 1)
        for q in range(parts):
            copy(q, t).wait_recv()
            first = mine(q, t) * half
            if t == steps - 1:
                outs[q][...] = source(q, t)[first].astype(F32) + got[q][t][0].astype(F32)
            else:
                def add(e, carry, q=q, t=t, first=first):
                    held[q][t][e] = (
                        source(q, t)[first + e].astype(F32) + got[q][t][e].astype(F32)
                    ).astype(BF)
                    return carry

                lax.fori_loop(0, half, add, 0)
                copy(q, t + 1).start()
    for t in range(steps):
        for q in range(parts):
            copy(q, t).wait_send()


def vmem():
    return pl.BlockSpec(memory_space=pltpu.VMEM)


def smem():
    return pl.BlockSpec(memory_space=pltpu.SMEM)


def hbm():
    return pl.BlockSpec(memory_space=pl.ANY)


def shape(dims, kind):
    return jax.ShapeDtypeStruct(dims, kind)


def flip(block, bit):
    n = lax.axis_size("client")
    return lax.ppermute(block, "client", [(i, i ^ (1 << bit)) for i in range(n)])


def per_device(
    patches, labels, assign, patch_embed, positions, client_in, client_down,
    server_in, server_down, classifier,
):
    n = lax.axis_size("client")
    group = n // SHARDS
    bits = group.bit_length() - 1
    me = lax.axis_index("client")
    rank = me % group
    rows = patches.shape[0]
    patch = patches.shape[1]
    width = client_in.shape[0]
    cols = client_in.shape[1]
    ff = client_down.shape[0]
    layers = server_in.shape[0]
    rows_in = server_in.shape[1]
    rows_down = server_down.shape[1]
    classes = classifier.shape[2]
    piece = rows // group
    per_image = IMG // group
    capacity = SLOTS * group
    s_rows = capacity * piece
    routes = assign.reshape(n)
    params = pltpu.CompilerParams(vmem_limit_bytes=VMEM_LIMIT)

    in_pieces = [server_in]
    down_pieces = [server_down]
    for bit in range(bits):
        in_pieces = in_pieces + [flip(p, bit) for p in in_pieces]
        down_pieces = down_pieces + [flip(p, bit) for p in down_pieces]

    slots, table = pl.pallas_call(
        functools.partial(gather_kernel, n, group, capacity),
        out_shape=[shape((s_rows, patch), BF), shape((capacity + 1,), jnp.int32)],
        in_specs=[smem(), vmem()],
        out_specs=[vmem(), smem()],
        scratch_shapes=[
            pltpu.VMEM((PLANE, group, piece, patch), BF),
            pltpu.VMEM((PLANE, capacity, piece, patch), BF),
            pltpu.VMEM((PLANE, capacity, piece, patch), BF),
            pltpu.SemaphoreType.DMA((group,)),
            pltpu.SemaphoreType.DMA((group,)),
            pltpu.SemaphoreType.DMA((PLANE, group)),
            pltpu.SemaphoreType.DMA((PLANE, group)),
            pltpu.SemaphoreType.DMA((PLANE,)),
            pltpu.SemaphoreType.DMA((PLANE,)),
        ],
        compiler_params=pltpu.CompilerParams(
            collective_id=1, has_side_effects=True, vmem_limit_bytes=VMEM_LIMIT
        ),
    )(routes, patches.reshape(group, piece, patch))

    def kept(r):
        return [
            shape((r, 3 * width), F32),
            shape((r // LANES * HEADS, LANES, LANES), BF),
            shape((r, width), BF),
            shape((r, width), F32),
            shape((r, ff), F32),
        ]

    r_in = cols // n
    head = split_rows(r_in)
    tall = [head, r_in - head + (ff // width - 1) * PAD, 2 * PAD]
    part_in = shape((layers, rows_in, cols), BF)
    part_down = shape((layers, rows_down, width), BF)
    res = pl.pallas_call(
        functools.partial(step_kernel, n, group, layers, per_image, capacity, classes),
        out_shape=[
            shape((1, capacity * per_image), F32),
            shape((width, classes), BF),
        ]
        + [shape((n, r, width), BF) for r in tall]
        + [part_in] * group
        + [part_down] * group,
        in_specs=[smem(), smem()] + [vmem()] * 3 + [hbm()] * (3 + 2 * group),
        out_specs=[vmem()] * 5 + [hbm()] * (2 * group),
        scratch_shapes=[
            pltpu.VMEM((layers + 1, width, cols), BF),
            pltpu.VMEM((layers + 1, ff, width), BF),
            pltpu.VMEM((layers, width, cols), BF),
            pltpu.VMEM((layers, ff, width), BF),
            pltpu.VMEM((layers + 2, s_rows, width), F32),
        ]
        + [pltpu.VMEM((layers + 1,) + s.shape, s.dtype) for s in kept(s_rows)]
        + [
            pltpu.VMEM((s_rows, 3 * width), BF),
            pltpu.VMEM((s_rows, width), F32),
            pltpu.VMEM((width, classes), BF),
            pltpu.SemaphoreType.DMA((layers, 2 * group)),
            pltpu.SemaphoreType.DMA((layers, 2 * group)),
            pltpu.SemaphoreType.DMA((3,)),
        ],
        compiler_params=params,
    )(
        table, labels, slots, patch_embed, positions, classifier, client_in, client_down,
        *in_pieces, *down_pieces,
    )
    losses, gclass = res[:2]
    packs = res[2:5]
    parts_in = list(res[5 : 5 + group])
    parts_down = list(res[5 + group :])

    half = group // 2
    while half:
        bit = half.bit_length() - 1
        parts_in = [
            parts_in[i].astype(F32) + flip(parts_in[i + half].astype(BF), bit).astype(F32)
            for i in range(half)
        ]
        parts_down = [
            parts_down[i].astype(F32) + flip(parts_down[i + half].astype(BF), bit).astype(F32)
            for i in range(half)
        ]
        half //= 2
    gsum = gclass.astype(F32)
    for bit in range(bits):
        gsum = gsum + flip(gsum.astype(BF), bit).astype(F32)
    grad_class = lax.dynamic_slice_in_dim(gsum, rank * rows_in, rows_in, 0)

    steps = bits_of(n)
    sums = pl.pallas_call(
        functools.partial(reduce_kernel, n),
        out_shape=[shape((r, width), F32) for r in tall],
        in_specs=[vmem()] * 3,
        out_specs=[vmem()] * 3,
        scratch_shapes=[
            pltpu.VMEM((n >> (t + 1), r, width), BF) for r in tall for t in range(steps)
        ]
        + [pltpu.VMEM((n >> (t + 1), r, width), BF) for r in tall for t in range(steps - 1)]
        + [
            pltpu.SemaphoreType.DMA((3, steps)),
            pltpu.SemaphoreType.DMA((3, steps)),
        ],
        compiler_params=pltpu.CompilerParams(
            collective_id=2, has_side_effects=True, vmem_limit_bytes=VMEM_LIMIT
        ),
    )(*packs)
    own = width // n
    extra = r_in - head
    grad_in = jnp.concatenate([sums[0], sums[1][:extra]], axis=0).T
    down = jnp.concatenate([sums[1][extra:], sums[2]], axis=0)
    down = down.reshape(ff // width + 1, PAD, width)[:, :own]
    grad_down = down[:-1].transpose(0, 2, 1).reshape(ff, own)
    last = down[-1].T
    return (
        losses,
        last[:patch],
        last[width - LANES : width - LANES + TOK],
        grad_in,
        grad_down,
        parts_in[0],
        parts_down[0],
        grad_class,
    )


def solution(mesh):
    whole = P()
    in_specs = (
        P("client", None), whole, whole, whole, whole, whole, whole,
        P(None, "client", None), P(None, "client", None), whole,
    )
    out_specs = (
        P("client", None), P(None, "client"), P(None, "client"), P(None, "client"),
        P(None, "client"), P(None, "client", None), P(None, "client", None), P("client", None),
    )
    return jax.shard_map(
        per_device, mesh=mesh, in_specs=in_specs, out_specs=out_specs, check_vma=False
    )
```

time: 266 us -> 132 us (0.50)
  the two profiles are of different devices: /device:TPU:15 before, /device:TPU:0 now
where the time goes in v1:
time: 132 us; the launch traced here: 131 us
  Pallas kernels  102 us (77%)
  local copies, waits for them, and re-layouts  17.7 us (13%)
  other arithmetic  9.95 us (8%)
    pallas_call x1, Pallas kernels, per_device(): pl.pallas_call(functools.partial(step_kernel, n, group, layers, per_image...  41.3 us
    pallas_call x1, Pallas kernels, per_device(): pl.pallas_call(functools.partial(reduce_kernel, n), out_shape=[shape((r,...  39.8 us
    pallas_call x1, Pallas kernels, per_device(): pl.pallas_call(functools.partial(gather_kernel, n, group, capacity), out_...  20.5 us
    unnamed x15, local copies, waits for them, and re-layouts  11.1 us
    add x1, other arithmetic, per_device(): parts_down[i].astype(F32)  3.06 us
    add x1, other arithmetic, per_device(): parts_in[i].astype(F32)  3.04 us
  transfers between devices with their start and end apart: 5, of which 0 were waited for; matrix products, arithmetic and copies ran while one was open for 17% of the time, Pallas kernels for 46%

profile of v1, /device:TPU:0, one launch (start us, length us, event | category | flops | bytes accessed | tf_op | source)
XLA Modules:
  0.0 131.1 jit_solution(867715389425970663)
XLA Ops:
  0.6 0.6 collective-permute-start
  1.2 0.1 collective-permute-start.1
  1.3 1.5 %copy.18 = bf16[128,192]{1,0:T(8,128)(2,1)} copy(bf16[128,192]{0,1:T(8,128)(2,1)} %param.10) | data formatting | bytes 98304 | tf_op args[0]
  2.8 2.4 %copy.19.refs_5_ = bf16[16,384,10]{2,1,0:T(8,128)(2,1)} copy(bf16[16,384,10]{1,0,2:T(8,128)(2,1)} %param.19) | data formatting | bytes 245760 | tf_op args[9]
  5.2 20.5 %shard_map.161 = (bf16[256,192]{1,0:T(8,128)(2,1)}, s32[5]{0:T(128)}) custom-call(s32[32]{0:T(128)} %bitcast.25, bf16[2,64,192]{2,1,0:T(8,128)(2,1)} %bitcast.23), custom_call_target="tpu_custom_call" | custom-call | tf_op jit(solution)/shard_map/pallas_call | solution.py:631
  25.7 0.0 collective-permute-done.1.refs_11_
  25.7 0.0 copy-start.3
  25.7 0.0 collective-permute-done.refs_9_
  25.7 0.0 copy-start.1
  25.7 1.0 copy-done.3
  26.7 0.8 copy-done.1
  27.5 41.3 %shard_map.162 = (f32[1,16]{1,0:T(1,128)}, bf16[384,10]{1,0:T(8,128)(2,1)}, bf16[32,80,384]{2,1,0:T(8,128)(2,1)}, bf16[32,64,384]{2,1,0:T(8,128)(2,1)}, bf16[32,...) custom-call(s32[5]{0:T(128)} %get-tuple-element.22.refs_0_, ...), custom_call_target="tpu_custom_call" | custom-call | tf_op jit(solution)/shard_map/pallas_call | solution.py:666
  68.8 0.1 collective-permute-start.2
  68.8 0.5 collective-permute-start.3
  69.3 0.0 copy-start.2
  69.3 39.8 %shard_map.163 = (f32[80,384]{1,0:T(8,128)}, f32[64,384]{1,0:T(8,128)}, f32[32,384]{1,0:T(8,128)}) custom-call(bf16[32,80,384]{2,1,0:T(8,128)(2,1)} %get-tuple-element.25.refs_0_, bf16[32,64,384]{2,1,0:T(8,128)(2,1)} %get-tuple-element.26.refs_1_, bf16[32,32,384]{2,1,0:T(8,128)(2,1)} %get-tuple-element.27.refs_2_), custom_call_target="tpu_custom_call" | custom-call | tf_op jit(solution)/shard_map/pallas_call | solution.py:721
  109.1 0.9 slice.21
  110.0 0.7 slice.25
  110.8 0.0 collective-permute-start.4
  110.8 0.8 pad_maximum_fusion
  111.6 0.6 slice_bitcast_fusion
  112.2 1.6 %maximum_bitcast_fusion = f32[384,96]{0,1:T(8,128)} fusion(f32[16,384]{1,0:T(8,128)S(1)} %slice.25, f32[80,384]{1,0:T(8,128)} %get-tuple-element.30), kind=kLoop, calls=%fused_computation.2 | loop fusion | flops 36864 | bytes 294912 | tf_op jit(solution)/shard_map/transpose | solution.py:740
  113.8 0.6 slice.27
  114.4 1.6 %copy.24 = f32[1,12,384]{1,2,0:T(8,128)} copy(f32[1,12,384]{2,1,0:T(8,128)} %slice.27) | data formatting | bytes 36864
  116.0 1.5 %slice.28 = f32[192,12]{1,0:T(8,128)} slice(f32[384,12]{1,0:T(8,128)} %bitcast.19), slice={[0:192], [0:12]} | slice | bytes 18432 | tf_op jit(solution)/shard_map/slice | solution.py:747
  117.5 1.3 slice.29
  118.8 1.6 %copy.22 = f32[192,12]{0,1:T(8,128)} copy(f32[192,12]{1,0:T(8,128)} %slice.28) | data formatting | bytes 18432
  120.4 0.9 copy.27
  121.3 0.6 copy.25
  122.0 0.0 collective-permute-done.4
  122.0 1.5 %convert_add_fusion.2 = f32[192,10]{1,0:T(8,128)} fusion(bf16[384,10]{1,0:T(8,128)(2,1)} %collective-permute-done.4, s32[]{:T(128)S(6)} %select_n.11, bf16[384,10]{1,0:T(8,128)(2,1)} %get-tuple-element.35), kind=kLoop, calls=%fused_computation.5 | loop fusion | flops 5760 | bytes 15364 | tf_op jit(solution)/shard_map/add | solution.py:717
  123.4 1.6 %copy.23 = f32[192,10]{0,1:T(8,128)} copy(f32[192,10]{1,0:T(8,128)} %convert_add_fusion.2) | data formatting | bytes 15360
  125.0 0.0 collective-permute-done.3
  125.0 0.0 copy-done.2
  125.0 0.0 copy-start
  125.0 3.1 %convert_add_fusion.1 = f32[2,768,384]{2,1,0:T(8,128)} fusion(bf16[2,768,384]{2,1,0:T(8,128)(2,1)} %collective-permute-done.3, bf16[2,768,384]{2,1,0:T(8,128)(2,1)S(1)} %copy-done.2), kind=kLoop, calls=%fused_computation.1 | loop fusion | flops 1769472 | bytes 4718592 | tf_op jit(solution)/shard_map/add | solution.py:711
  128.1 0.0 collective-permute-done.2
  128.1 0.0 copy-done
  128.1 3.0 %convert_add_fusion = f32[2,192,3072]{2,1,0:T(8,128)} fusion(bf16[2,192,3072]{2,1,0:T(8,128)(2,1)S(1)} %collective-permute-done.2, bf16[2,192,3072]{2,1,0:T(8,128)(2,1)S(1)} %copy-done), kind=kLoop, calls=%fused_computation | loop fusion | flops 3538944 | bytes 9437184 | tf_op jit(solution)/shard_map/add | solution.py:707
  (1 shorter events, 0.0 us)
Async XLA Ops:
  0.6 25.1 %collective-permute-start = (bf16[2,192,3072]{2,1,0:T(8,128)(2,1)}, bf16[2,192,3072]{2,1,0:T(8,128)(2,1)S(1)}, u32[]{:S(2)}, u32[]{:S(2)}) collective-permute-start(bf16[2,192,3072]{2,1,0:T(8,128)(2,1)} %refs_8_.1), channel_id=1, source_target_pairs={{0,1},{1,0},{2,3},{3,2},{4,5},{5,4},{6,7},{7,6},{8,9},{9,8},{10,11... | collective-permute-start | bytes 7077896 | tf_op jit(solution)/shard_map/ppermute | solution.py:597
  1.2 24.5 %collective-permute-start.1 = (bf16[2,768,384]{2,1,0:T(8,128)(2,1)}, bf16[2,768,384]{2,1,0:T(8,128)(2,1)S(1)}, u32[]{:S(2)}, u32[]{:S(2)}) collective-permute-start(bf16[2,768,384]{2,1,0:T(8,128)(2,1)} %refs_10_.1), channel_id=1, source_target_pairs={{0,1},{1,0},{2,3},{3,2},{4,5},{5,4},{6,7},{7,6},{8,9},{9,8},{10,11... | collective-permute-start | bytes 3538952 | tf_op jit(solution)/shard_map/ppermute | solution.py:597
  25.7 1.0 copy-start.3
  25.7 1.8 %copy-start.1 = (bf16[2,192,3072]{2,1,0:T(8,128)(2,1)}, bf16[2,192,3072]{2,1,0:T(8,128)(2,1)S(1)}, u32[]{:S(2)}) copy-start(bf16[2,192,3072]{2,1,0:T(8,128)(2,1)S(1)} %collective-permute-done.refs_9_) | copy-start | bytes 7077892
  68.8 59.3 %collective-permute-start.2 = (bf16[2,192,3072]{2,1,0:T(8,128)(2,1)}, bf16[2,192,3072]{2,1,0:T(8,128)(2,1)S(1)}, u32[]{:S(2)}, u32[]{:S(2)}) collective-permute-start(bf16[2,192,3072]{2,1,0:T(8,128)(2,1)} %get-tuple-element.32), channel_id=1, source_target_pairs={{0,1},{1,0},{2,3},{3,2},{4,5},{5,4},{6,7},{7,6},{8,9},{9,8},{10,11... | collective-permute-start | bytes 7077896 | tf_op jit(solution)/shard_map/ppermute | solution.py:597
  68.8 56.2 %collective-permute-start.3 = (bf16[2,768,384]{2,1,0:T(8,128)(2,1)}, bf16[2,768,384]{2,1,0:T(8,128)(2,1)}, u32[]{:S(2)}, u32[]{:S(2)}) collective-permute-start(bf16[2,768,384]{2,1,0:T(8,128)(2,1)} %get-tuple-element.34), channel_id=1, source_target_pairs={{0,1},{1,0},{2,3},{3,2},{4,5},{5,4},{6,7},{7,6},{8,9},{9,8},{10,11... | collective-permute-start | bytes 3538952 | tf_op jit(solution)/shard_map/ppermute | solution.py:597
  69.3 55.7 %copy-start.2 = (bf16[2,768,384]{2,1,0:T(8,128)(2,1)S(1)}, bf16[2,768,384]{2,1,0:T(8,128)(2,1)}, u32[]{:S(2)}) copy-start(bf16[2,768,384]{2,1,0:T(8,128)(2,1)} %get-tuple-element.33) | copy-start | bytes 3538948
  110.8 11.2 %collective-permute-start.4 = (bf16[384,10]{1,0:T(8,128)(2,1)}, bf16[384,10]{1,0:T(8,128)(2,1)}, u32[]{:S(2)}, u32[]{:S(2)}) collective-permute-start(bf16[384,10]{1,0:T(8,128)(2,1)} %get-tuple-element.35), channel_id=1, source_target_pairs={{0,1},{1,0},{2,3},{3,2},{4,5},{5,4},{6,7},{7,6},{8,9},{9,8},{10,11... | collective-permute-start | bytes 23048 | tf_op jit(solution)/shard_map/ppermute | solution.py:597
  125.0 3.1 %copy-start = (bf16[2,192,3072]{2,1,0:T(8,128)(2,1)S(1)}, bf16[2,192,3072]{2,1,0:T(8,128)(2,1)}, u32[]{:S(2)}) copy-start(bf16[2,192,3072]{2,1,0:T(8,128)(2,1)} %get-tuple-element.31) | copy-start | bytes 7077892

commit v2 on v1

v2 whole, which is shorter than its diff:
```python
import functools
import math

import jax
import jax.numpy as jnp
from jax import lax
from jax.experimental import pallas as pl
from jax.experimental.pallas import tpu as pltpu
from jax.sharding import PartitionSpec as P

HEADS = 6
TOK = 16
IMG = 8
SHARDS = 16
SLOTS = 2
PLANE = 4
EPSILON = 1e-06
LANES = 128
PAD = 16
BF = jnp.bfloat16
F32 = jnp.float32
HIGH = lax.Precision.HIGHEST
GELU_C = math.sqrt(2.0 / math.pi)
VMEM_LIMIT = 60 * 1024 * 1024
MESH = pl.DeviceIdType.MESH


def mm(a, b, precision=None):
    return lax.dot_general(
        a, b, (((1,), (0,)), ((), ())), precision=precision, preferred_element_type=F32
    )


def mm_nt(a, b, precision=None):
    return lax.dot_general(
        a, b, (((1,), (1,)), ((), ())), precision=precision, preferred_element_type=F32
    )


def mm_tn(a, b):
    return lax.dot_general(a, b, (((0,), (0,)), ((), ())), preferred_element_type=F32)


def norm(v):
    centre = v - jnp.mean(v, axis=-1, keepdims=True)
    scale = lax.rsqrt(jnp.mean(centre * centre, axis=-1, keepdims=True) + EPSILON)
    return centre * scale, scale


def norm_back(normed, scale, grad):
    return scale * (
        grad
        - jnp.mean(grad, axis=-1, keepdims=True)
        - normed * jnp.mean(grad * normed, axis=-1, keepdims=True)
    )


def gelu_both(v):
    sq = v * v
    t = jnp.tanh(v * (GELU_C + (GELU_C * 0.044715) * sq))
    half = 0.5 + 0.5 * t
    slope = half + (0.5 * v) * (1.0 - t * t) * (GELU_C + (GELU_C * 0.134145) * sq)
    return v * half, slope


def image_mask(per):
    row = lax.broadcasted_iota(jnp.int32, (per * LANES, LANES), 0) % LANES
    col = lax.broadcasted_iota(jnp.int32, (per * LANES, LANES), 1)
    return row // TOK == col // TOK


def lane_masks(head_dim):
    lane = lax.broadcasted_iota(jnp.int32, (LANES, LANES), 1)
    return [lane // head_dim == h for h in range(LANES // head_dim)]


def stack(value, keeps):
    return jnp.concatenate([jnp.where(k, value, jnp.zeros_like(value)) for k in keeps], axis=0)


def widen(value, per):
    return jnp.concatenate(
        [value[h * LANES : (h + 1) * LANES] for h in range(per)], axis=1
    )


def attend(qkv_ref, probs_ref, att_ref, width):
    rows = qkv_ref.shape[0]
    head_dim = width // HEADS
    per = LANES // head_dim
    inside = image_mask(per)
    keeps = lane_masks(head_dim)
    for group in range(rows // LANES):
        r = slice(group * LANES, (group + 1) * LANES)
        for pair in range(width // LANES):
            lo = pair * LANES
            q = qkv_ref[r, lo : lo + LANES]
            k = qkv_ref[r, width + lo : width + lo + LANES]
            v = qkv_ref[r, 2 * width + lo : 2 * width + lo + LANES]
            s = jnp.where(inside, mm_nt(stack(q, keeps), k), -1e30)
            e = jnp.exp(s - jnp.max(s, axis=-1, keepdims=True))
            p = (e * (1.0 / jnp.sum(e, axis=-1, keepdims=True))).astype(BF)
            probs_ref[group * (width // LANES) + pair] = p
            att_ref[r, lo : lo + LANES] = mm(widen(p, per), stack(v, keeps)).astype(BF)


def attend_back(grad, qkv_ref, probs_ref, dqkv_ref, width):
    rows = qkv_ref.shape[0]
    head_dim = width // HEADS
    per = LANES // head_dim
    keeps = lane_masks(head_dim)
    for group in range(rows // LANES):
        r = slice(group * LANES, (group + 1) * LANES)
        for pair in range(width // LANES):
            lo = pair * LANES
            q = qkv_ref[r, lo : lo + LANES]
            k = qkv_ref[r, width + lo : width + lo + LANES]
            v = qkv_ref[r, 2 * width + lo : 2 * width + lo + LANES]
            go = stack(grad[r, lo : lo + LANES].astype(BF), keeps)
            p = probs_ref[group * (width // LANES) + pair]
            dp = mm_nt(go, v)
            dv = mm_tn(p, go)
            pf = p.astype(F32)
            ds = (pf * (dp - jnp.sum(pf * dp, axis=-1, keepdims=True))).astype(BF)
            dq = mm(widen(ds, per), stack(k, keeps)) * (1.0 / math.sqrt(head_dim))
            dk = mm_tn(ds, stack(q, keeps))
            dqkv_ref[r, lo : lo + LANES] = dq.astype(BF)
            dqkv_ref[r, width + lo : width + lo + LANES] = dk.astype(BF)
            dqkv_ref[r, 2 * width + lo : 2 * width + lo + LANES] = dv.astype(BF)


def block_forward(x, w_ref, d_ref, first, qkv_ref, probs_ref, att_ref, second, h_ref, slope_ref):
    width = x.shape[1]
    ff = d_ref.shape[0]
    u, scale = norm(x)
    u = u.astype(BF)
    first[0][...] = u
    first[1][...] = scale
    for part in range(3):
        value = mm(u, w_ref[:, part * width : (part + 1) * width])
        if part == 0:
            value = value * (1.0 / math.sqrt(width // HEADS))
        qkv_ref[:, part * width : (part + 1) * width] = value.astype(BF)
    attend(qkv_ref, probs_ref, att_ref, width)
    y = x + mm(att_ref[...], w_ref[:, 3 * width : 4 * width])
    u, scale = norm(y)
    u = u.astype(BF)
    second[0][...] = u
    second[1][...] = scale
    for lo in range(0, ff, width):
        value, slope = gelu_both(mm(u, w_ref[:, 4 * width + lo : 5 * width + lo]))
        h_ref[:, lo : lo + width] = value.astype(BF)
        slope_ref[:, lo : lo + width] = slope.astype(BF)
    return y + mm(h_ref[...], d_ref[...])


def block_backward(
    g, w_ref, d_ref, first, qkv_ref, probs_ref, att_ref, second, h_ref, slope_ref, dqkv_ref,
    put_in, put_down, after=lambda stage: None,
):
    width = g.shape[1]
    ff = d_ref.shape[0]
    gb = g.astype(BF)
    put_down(h_ref, gb)
    after(0)
    for lo in range(0, ff, width):
        slope = slope_ref[:, lo : lo + width].astype(F32)
        slope_ref[:, lo : lo + width] = (mm_nt(gb, d_ref[lo : lo + width, :]) * slope).astype(BF)
    put_in(4 * width, second[0], slope_ref)
    after(1)
    dy = g + norm_back(
        second[0][...].astype(F32), second[1][...], mm_nt(slope_ref[...], w_ref[:, 4 * width :])
    )
    gb = dy.astype(BF)
    dqkv_ref[:, :width] = gb
    put_in(3 * width, att_ref, dqkv_ref.at[:, :width])
    after(2)
    attend_back(
        mm_nt(gb, w_ref[:, 3 * width : 4 * width]), qkv_ref, probs_ref, dqkv_ref, width
    )
    after(3)
    put_in(0, first[0], dqkv_ref)
    after(4)
    return dy + norm_back(
        first[0][...].astype(F32), first[1][...], mm_nt(dqkv_ref[...], w_ref[:, : 3 * width])
    )


def bits_of(n):
    return n.bit_length() - 1


def place_of(device, order):
    index = 0
    for bit in order:
        index = index * 2 + (device >> bit & 1)
    return index


def pad_of(own):
    return (own + 7) // 8 * 8


def chain_plan(n, r_in, blocks, pad):
    steps = bits_of(n)
    rest = list(range(1, steps))
    far = rest[-2:]
    near = rest[:-2]
    low = near[: len(near) // 2]
    high = near[len(near) // 2 :]
    first = [0] + low + high + far
    second = [0] + high + low + far
    third = [0] + far + low + high
    top = (r_in // 2 + PAD - 1) // PAD * PAD
    half = blocks // 2 * pad
    return [
        (half, first), (blocks * pad - half, second),
        (top, first[:-1]), (r_in - top, second[:-1]),
        (top, first[:-1]), (r_in - top, second[:-1]),
        (pad, third),
    ]


DOWN, UPPER, LOWER, LAST = 0, 2, 4, 6


def step_kernel(n, group, layers, per_image, capacity, classes, plan, *refs):
    (
        assign_hbm, label_hbm, turned_hbm, embed_hbm, pos_hbm, class_hbm,
        cin_hbm, cdown_hbm, sin_hbm, sdown_hbm,
    ) = refs[:10]
    refs = refs[10:]
    loss_ref, gclass_ref, gin_sum, gdown_sum, cin_sum, down_first, down_second, last_sum = refs[:8]
    refs = refs[8:]
    (
        assign_ref, label_ref, turned_ref, embed_ref, pos_ref, class_ref,
        patch_ref, column, pack, got_slots, slots_ref,
        first_u, first_s, qkv, probs, att, second_u, second_s, hidden,
        slope, dqkv, gcur,
        gclass_own, gclass_got, joined, joined_got,
    ) = refs[:26]
    refs = refs[26:]
    wbuf, dbuf, refs = refs[: layers + 1], refs[layers + 1 : 2 * layers + 2], refs[2 * layers + 2 :]
    gin, gdown, refs = refs[:layers], refs[layers : 2 * layers], refs[2 * layers :]
    gin_got, gdown_got, refs = refs[:layers], refs[layers : 2 * layers], refs[2 * layers :]
    chains = len(plan)
    packs, refs = refs[:chains], refs[chains:]
    got, held = [], []
    for rows, order in plan:
        count = len(order)
        got.append(refs[:count])
        held.append(refs[count : 2 * count - 1])
        refs = refs[2 * count - 1 :]
    (
        load_sem, own_sem, near_send, near_recv, far_send, far_recv, flat_send, flat_recv,
        w_send, w_recv, g_send, g_recv, c_send, c_recv, r_send, r_recv, j_send, j_recv,
    ) = refs
    steps = bits_of(n)
    me = lax.axis_index("client")
    rank = me % group
    shard = me // group
    line = shard // PLANE
    spot = shard % PLANE
    rows_in = sin_hbm.shape[1]
    rows_down = sdown_hbm.shape[1]
    rows, width = gcur.shape
    ff = dbuf[0].shape[0]

    loads = [
        pltpu.make_async_copy(source, target, load_sem.at[i])
        for i, (source, target) in enumerate([
            (turned_hbm, turned_ref), (assign_hbm, assign_ref), (label_hbm, label_ref),
            (embed_hbm, embed_ref), (pos_hbm, pos_ref), (class_hbm, class_ref),
            (cin_hbm, wbuf[0]), (cdown_hbm, dbuf[0]),
        ])
    ]
    for c in loads:
        c.start()

    def own_in(layer):
        return pltpu.make_async_copy(
            sin_hbm.at[layer],
            wbuf[layer + 1].at[pl.ds(rank * rows_in, rows_in)],
            own_sem.at[layer, 0],
        )

    def own_down(layer):
        return pltpu.make_async_copy(
            sdown_hbm.at[layer],
            dbuf[layer + 1].at[pl.ds(rank * rows_down, rows_down)],
            own_sem.at[layer, 1],
        )

    def near_peer(i):
        return shard * group + lax.rem(rank + i, group)

    def far_peer(i):
        return (lax.rem(line + i, PLANE) * PLANE + spot) * group + rank

    def flat_peer(i):
        return (line * PLANE + lax.rem(spot + i, PLANE)) * group + rank

    def remote(source, target, send, recv, peer):
        return pltpu.make_async_remote_copy(
            src_ref=source, dst_ref=target, send_sem=send, recv_sem=recv,
            device_id=(peer,), device_id_type=MESH,
        )

    def near(i):
        to = lax.rem(rank + i, group)
        return remote(
            patch_ref.at[to], column.at[line, rank], near_send.at[i], near_recv.at[i], near_peer(i)
        )

    def far(i, j):
        if j == 0:
            source, member = patch_ref.at[rank], rank
        else:
            member = lax.rem(rank + group - j, group)
            source = column.at[line, member]
        return remote(
            source, column.at[line, member], far_send.at[i, j], far_recv.at[i, j], far_peer(i)
        )

    def flat(i):
        return remote(
            pack.at[i], got_slots.at[spot], flat_send.at[i], flat_recv.at[i], flat_peer(i)
        )

    def weight_in(layer, i):
        return remote(
            sin_hbm.at[layer],
            wbuf[layer + 1].at[pl.ds(rank * rows_in, rows_in)],
            w_send.at[layer, i, 0], w_recv.at[layer, i, 0], near_peer(i),
        )

    def weight_down(layer, i):
        return remote(
            sdown_hbm.at[layer],
            dbuf[layer + 1].at[pl.ds(rank * rows_down, rows_down)],
            w_send.at[layer, i, 1], w_recv.at[layer, i, 1], near_peer(i),
        )

    def grad_in(layer, i):
        to = lax.rem(rank + i, group)
        return remote(
            gin[layer].at[pl.ds(to * rows_in, rows_in)],
            gin_got[layer].at[i - 1], g_send.at[layer, i, 0], g_recv.at[layer, i, 0], near_peer(i),
        )

    def grad_down(layer, i):
        to = lax.rem(rank + i, group)
        return remote(
            gdown[layer].at[pl.ds(to * rows_down, rows_down)],
            gdown_got[layer].at[i - 1], g_send.at[layer, i, 1], g_recv.at[layer, i, 1],
            near_peer(i),
        )

    def grad_class(i):
        return remote(gclass_own, gclass_got.at[i - 1], c_send.at[i], c_recv.at[i], near_peer(i))

    barrier = pltpu.get_barrier_semaphore()
    peers = [near_peer(i) for i in range(1, group)]
    peers += [far_peer(i) for i in range(1, PLANE)]
    peers += [flat_peer(i) for i in range(1, PLANE)]
    for peer in peers:
        pl.semaphore_signal(barrier, inc=1, device_id=(peer,), device_id_type=MESH)
    for layer in range(layers):
        own_in(layer).start()
        own_down(layer).start()
    loads[0].wait()
    patch_ref[...] = turned_ref[...].astype(F32).T.astype(BF).reshape(patch_ref.shape)
    pl.semaphore_wait(barrier, len(peers))

    for i in range(1, group):
        near(i).start()
    for i in range(1, PLANE):
        far(i, 0).start()
    for layer in range(layers):
        for i in range(1, group):
            weight_in(layer, i).start()
            weight_down(layer, i).start()
    for j in range(1, group):
        near(j).wait_recv()
        for i in range(1, PLANE):
            far(i, j).start()
    column[line, rank] = patch_ref[rank]

    targets = [line * PLANE + lax.rem(spot + i, PLANE) for i in range(PLANE)]
    loads[1].wait()
    loads[2].wait()

    def scan(c, carry):
        there = assign_ref[c]
        out = []
        for i in range(PLANE):
            count, slots = carry[i]
            hit = there == targets[i]
            slots = tuple(
                jnp.where(hit & (count == k), c, slots[k]) for k in range(capacity)
            )
            out.append((count + jnp.where(hit, 1, 0), slots))
        return tuple(out)

    zero = jnp.int32(0)
    table = lax.fori_loop(
        0, n, scan, tuple((zero, tuple(zero for _ in range(capacity))) for _ in range(PLANE))
    )
    filled, slots = table[0]
    images = capacity * per_image
    row = lax.broadcasted_iota(jnp.int32, (images, classes), 0)
    lane = lax.broadcasted_iota(jnp.int32, (images, classes), 1)
    want = jnp.full((images, classes), -1, jnp.int32)
    for k in range(capacity):
        base = slots[k] * (group * per_image) + rank * per_image
        for j in range(per_image):
            lab = jnp.where(k < filled, label_ref[base + j], -1)
            want = jnp.where(row == k * per_image + j, lab, want)
    hot = (lane == want).astype(F32)
    full = (want[:, :1] >= 0).astype(F32)
    loads[5].wait()
    every = class_ref[...].astype(F32)
    chosen = lax.broadcasted_iota(jnp.int32, every.shape, 1) == shard
    cls = jnp.sum(jnp.where(chosen, every, 0.0), axis=1).astype(BF)

    for i in range(1, PLANE):
        for j in range(group):
            far(i, j).wait_recv()

    def pick(c):
        home = c // group
        return column[home // PLANE, c % group]

    for i in range(1, PLANE):
        for k in range(capacity):
            pack[i, k] = pick(table[i][1][k])
        flat(i).start()
    for k in range(capacity):
        got_slots[spot, k] = pick(slots[k])
    for c in (3, 4, 6, 7):
        loads[c].wait()
    for i in range(1, PLANE):
        flat(i).wait_recv()
    piece = patch_ref.shape[1]
    for k in range(capacity):
        home = slots[k] // group
        slots_ref[k * piece : (k + 1) * piece, :] = got_slots[home % PLANE, k]

    x = mm(slots_ref[...], embed_ref[...])
    pos = pos_ref[...].astype(F32)
    gcur[...] = x + jnp.concatenate([pos] * (rows // TOK), axis=0)

    def saved(layer):
        return (
            (first_u.at[layer], first_s.at[layer]), qkv.at[layer], probs.at[layer], att.at[layer],
            (second_u.at[layer], second_s.at[layer]), hidden.at[layer], slope.at[layer],
        )

    for layer in range(layers + 1):
        if layer > 0:
            own_in(layer - 1).wait()
            own_down(layer - 1).wait()
            for i in range(1, group):
                weight_in(layer - 1, i).wait_recv()
                weight_down(layer - 1, i).wait_recv()

        out = block_forward(gcur[...], wbuf[layer], dbuf[layer], *saved(layer))
        gcur[...] = out if layer else out.astype(BF).astype(F32)

    pool = (
        lax.broadcasted_iota(jnp.int32, (images, rows), 1) // TOK
        == lax.broadcasted_iota(jnp.int32, (images, rows), 0)
    ).astype(F32) * (1.0 / TOK)
    unpool = (
        lax.broadcasted_iota(jnp.int32, (rows, images), 0) // TOK
        == lax.broadcasted_iota(jnp.int32, (rows, images), 1)
    ).astype(F32) * (1.0 / TOK)
    u, scale = norm(mm(pool, gcur[...], HIGH))
    pooled = u.astype(BF)
    logits = mm_nt(pooled, cls)
    top = jnp.max(logits, axis=-1, keepdims=True)
    e = jnp.exp(logits - top)
    total = jnp.sum(e, axis=-1, keepdims=True)
    loss = (
        jnp.log(total) + top - jnp.sum(jnp.where(lane == want, logits, 0.0), axis=-1, keepdims=True)
    ) * full
    eye = (
        lax.broadcasted_iota(jnp.int32, (images, images), 0)
        == lax.broadcasted_iota(jnp.int32, (images, images), 1)
    )
    loss_ref[...] = jnp.sum(jnp.where(eye, loss, 0.0), axis=0, keepdims=True)
    dlog = ((e / total - hot) * full).astype(BF)
    gclass_own[...] = mm_tn(dlog, pooled).astype(BF)
    for i in range(1, group):
        grad_class(i).start()
    dpool = norm_back(u, scale, mm(dlog, cls))
    gcur[...] = mm(unpool, dpool, HIGH)

    for layer in reversed(range(layers)):
        def put_in(start, lhs, rhs, layer=layer):
            for c in range(0, rhs.shape[1], width):
                gin[layer][:, start + c : start + c + width] = mm_tn(
                    lhs[...], rhs[:, c : c + width]
                ).astype(BF)

        def put_down(h, gb, layer=layer):
            for c in range(0, ff, width):
                gdown[layer][c : c + width] = mm_tn(h[:, c : c + width], gb).astype(BF)

        deep = layer + 1
        gcur[...] = block_backward(
            gcur[...], wbuf[deep], dbuf[deep], *saved(deep), dqkv, put_in, put_down,
        )
        for i in range(1, group):
            grad_down(layer, i).start()
            grad_in(layer, i).start()

    def peer_of(bit):
        return me + (1 << bit) - 2 * (1 << bit) * (me // (1 << bit) % 2)

    def mine(bit):
        return me // (1 << bit) % 2

    def source(c, t):
        return packs[c] if t == 0 else held[c][t - 1]

    def size_at(c, t):
        return packs[c].shape[0] >> (t + 1)

    def copy(c, t):
        bit = plan[c][1][t]
        half = size_at(c, t)
        return remote(
            source(c, t).at[pl.ds((1 - mine(bit)) * half, half)], got[c][t],
            r_send.at[c, t], r_recv.at[c, t], peer_of(bit),
        )

    def join(c):
        bit = steps - 1
        take = plan[UPPER + c][0]
        return remote(
            joined.at[c, 1 - mine(bit), pl.ds(0, take)], joined_got.at[c, pl.ds(0, take)],
            j_send.at[c], j_recv.at[c], peer_of(bit),
        )

    def store_final(c, value):
        if c == LAST:
            last_sum[...] = value
        elif c == DOWN:
            down_first[...] = value
        elif c == DOWN + 1:
            down_second[...] = value
        else:
            side = 1 if c < LOWER else 0
            joined[c % 2, side, : value.shape[0]] = value.astype(BF)

    progress = [0] * chains

    def advance(c):
        t = progress[c]
        count = len(plan[c][1])
        if t >= count:
            return
        progress[c] = t + 1
        half = size_at(c, t)
        copy(c, t).wait_recv()
        first = mine(plan[c][1][t]) * half
        if t == count - 1:
            store_final(c, source(c, t)[first].astype(F32) + got[c][t][0].astype(F32))
            return

        def add(e, carry):
            held[c][t][e] = (
                source(c, t)[first + e].astype(F32) + got[c][t][e].astype(F32)
            ).astype(BF)
            return carry

        lax.fori_loop(0, half, add, 0)
        copy(c, t + 1).start()

    per_dev = wbuf[0].shape[1] // n
    cols = width // n
    pad = pad_of(cols)
    src = lax.broadcasted_iota(jnp.int32, (width, n * pad), 0)
    dst = lax.broadcasted_iota(jnp.int32, (width, n * pad), 1)
    spread_to = ((dst // pad == src // cols) & (dst % pad == src % cols)).astype(F32).astype(BF)
    tok = (
        lax.broadcasted_iota(jnp.int32, (rows, LANES), 0) % TOK
        == lax.broadcasted_iota(jnp.int32, (rows, LANES), 1)
    ).astype(F32).astype(BF)

    def put_in(start, lhs, rhs):
        base = UPPER if start >= 4 * width else LOWER
        for c in range(0, rhs.shape[1], width):
            part = mm_tn(rhs[:, c : c + width], lhs[...]).astype(BF)
            first = (start + c) // per_dev
            for j in range(width // per_dev):
                lo = j * per_dev
                for piece_at in range(2):
                    take, order = plan[base + piece_at]
                    packs[base + piece_at][place_of(first + j, order)] = part[lo : lo + take]
                    lo += take

    def put_down(h, gb):
        spread = mm(gb, spread_to).astype(BF)
        for q in range(ff // width):
            part = mm_tn(spread, h[:, q * width : (q + 1) * width]).astype(BF)
            c = DOWN if q * pad < plan[DOWN][0] else DOWN + 1
            lo = q * pad if c == DOWN else q * pad - plan[DOWN][0]
            for j in range(n):
                packs[c][place_of(j, plan[c][1]), lo : lo + pad] = part[j * pad : (j + 1) * pad]

    def after(stage):
        if stage == 0:
            copy(DOWN, 0).start()
            copy(DOWN + 1, 0).start()
        elif stage == 1:
            copy(UPPER, 0).start()
            copy(UPPER + 1, 0).start()
            advance(DOWN)
            advance(DOWN + 1)
        elif stage == 2:
            advance(UPPER)
            advance(UPPER + 1)
        elif stage == 3:
            advance(DOWN)
            advance(DOWN + 1)
        else:
            copy(LOWER, 0).start()
            copy(LOWER + 1, 0).start()

    dx = block_backward(
        gcur[...].astype(BF).astype(F32), wbuf[0], dbuf[0], *saved(0), dqkv,
        put_in, put_down, after,
    )
    spread = mm(dx.astype(BF), spread_to).astype(BF)
    patch = slots_ref.shape[1]
    embed_part = mm_tn(spread, slots_ref[...]).astype(BF)
    pos_part = mm_tn(spread, tok).astype(BF)
    for j in range(n):
        at = place_of(j, plan[LAST][1])
        packs[LAST][at, :, :patch] = embed_part[j * pad : (j + 1) * pad]
        packs[LAST][at, :, patch : width - LANES] = jnp.zeros((pad, width - LANES - patch), BF)
        packs[LAST][at, :, width - LANES :] = pos_part[j * pad : (j + 1) * pad]
    copy(LAST, 0).start()

    def add_layer(layer):
        for i in range(1, group):
            grad_down(layer, i).wait_recv()
            grad_in(layer, i).wait_recv()
        start = rank * rows_in
        whole = gin[layer][pl.ds(start, rows_in)].astype(F32)
        for i in range(1, group):
            whole = whole + gin_got[layer][i - 1].astype(F32)
        gin_sum[layer] = whole.astype(BF)
        start = rank * rows_down
        whole = gdown[layer][pl.ds(start, rows_down)].astype(F32)
        for i in range(1, group):
            whole = whole + gdown_got[layer][i - 1].astype(F32)
        gdown_sum[layer] = whole.astype(BF)

    rounds = 0
    while any(progress[c] < len(plan[c][1]) for c in range(chains)):
        for c in (LOWER, LOWER + 1, UPPER, UPPER + 1, LAST, DOWN, DOWN + 1):
            done = progress[c] == len(plan[c][1])
            advance(c)
            if LOWER <= c < LAST and not done and progress[c] == len(plan[c][1]):
                other = c - LOWER + UPPER
                while progress[other] < len(plan[other][1]):
                    advance(other)
                join(c - LOWER).start()
        if rounds < layers:
            add_layer(layers - 1 - rounds)
        rounds += 1
    for i in range(1, group):
        grad_class(i).wait_recv()
    both = gclass_own[...].astype(F32)
    for i in range(1, group):
        both = both + gclass_got[i - 1].astype(F32)
    kept = both[:, :rows_in]
    for i in range(1, group):
        kept = jnp.where(rank == i, both[:, i * rows_in : (i + 1) * rows_in], kept)
    gclass_ref[...] = kept
    lo = 0
    for c in range(2):
        join(c).wait_recv()
        take = plan[UPPER + c][0]
        cin_sum[lo : lo + take, :] = (
            joined[c, mine(steps - 1), :take].astype(F32) + joined_got[c, :take].astype(F32)
        )
        lo += take

    for i in range(1, group):
        near(i).wait_send()
        grad_class(i).wait_send()
        for layer in range(layers):
            weight_in(layer, i).wait_send()
            weight_down(layer, i).wait_send()
            grad_in(layer, i).wait_send()
            grad_down(layer, i).wait_send()
    for i in range(1, PLANE):
        flat(i).wait_send()
        for j in range(group):
            far(i, j).wait_send()
    for c in range(chains):
        for t in range(len(plan[c][1])):
            copy(c, t).wait_send()
    for c in range(2):
        join(c).wait_send()


def finish_kernel(
    near_in, near_down, class_ref, loss_in, cin_sum, down_first, down_second, last_sum,
    gin_ref, gdown_ref, gclass_ref, loss_ref, cin_ref, cdown_ref, embed_ref, pos_ref,
):
    gin_ref[...] = near_in[...].astype(F32)
    gdown_ref[...] = near_down[...].astype(F32)

    @pl.when((pl.program_id(0) == 0) & (pl.program_id(1) == 0))
    def _():
        gclass_ref[...] = class_ref[...]
        loss_ref[...] = loss_in[...]
        cin_ref[...] = cin_sum[...]
        own, width = cdown_ref.shape[0], cin_sum.shape[1]
        pad = pad_of(own)
        q = 0
        for part in (down_first, down_second):
            for lo in range(0, part.shape[0], pad):
                cdown_ref[:, q * width : (q + 1) * width] = part[lo : lo + pad, :][:own]
                q += 1
        last = last_sum[...]
        embed_ref[...] = last[:own, : embed_ref.shape[1]]
        pos_ref[...] = last[:, width - LANES :].T[:TOK, :own]


def vmem():
    return pl.BlockSpec(memory_space=pltpu.VMEM)


def hbm():
    return pl.BlockSpec(memory_space=pltpu.HBM)


def shape(dims, kind):
    return jax.ShapeDtypeStruct(dims, kind)


def per_device(
    patches, labels, assign, patch_embed, positions, client_in, client_down,
    server_in, server_down, classifier,
):
    n = lax.axis_size("client")
    group = n // SHARDS
    rows = patches.shape[0]
    patch = patches.shape[1]
    width = client_in.shape[0]
    cols = client_in.shape[1]
    ff = client_down.shape[0]
    layers = server_in.shape[0]
    rows_in = server_in.shape[1]
    rows_down = server_down.shape[1]
    classes = classifier.shape[2]
    piece = rows // group
    per_image = IMG // group
    capacity = SLOTS * group
    s_rows = capacity * piece
    r_in = cols // n
    own = width // n
    steps = bits_of(n)
    pad = pad_of(own)
    plan = chain_plan(n, r_in, ff // width, pad)
    shards = classifier.shape[0]
    per = LANES // (width // HEADS)
    spaces = [
        ((s_rows, width), BF),
        ((s_rows, 1), F32),
        ((s_rows, 3 * width), BF),
        ((s_rows // LANES * (width // LANES), per * LANES, LANES), BF),
        ((s_rows, width), BF),
        ((s_rows, width), BF),
        ((s_rows, 1), F32),
        ((s_rows, ff), BF),
        ((s_rows, ff), BF),
    ]
    scratch = [
        pltpu.SMEM((n,), jnp.int32),
        pltpu.SMEM((n * IMG,), jnp.int32),
        pltpu.VMEM((patch, rows), BF),
        pltpu.VMEM((patch, width), BF),
        pltpu.VMEM((TOK, width), BF),
        pltpu.VMEM((classes, shards, width), BF),
        pltpu.VMEM((group, piece, patch), BF),
        pltpu.VMEM((PLANE, group, piece, patch), BF),
        pltpu.VMEM((PLANE, capacity, piece, patch), BF),
        pltpu.VMEM((PLANE, capacity, piece, patch), BF),
        pltpu.VMEM((s_rows, patch), BF),
    ]
    scratch += [pltpu.VMEM((layers + 1,) + dims, kind) for dims, kind in spaces]
    scratch += [
        pltpu.VMEM((s_rows, 3 * width), BF),
        pltpu.VMEM((s_rows, width), F32),
        pltpu.VMEM((classes, width), BF),
        pltpu.VMEM((group - 1, classes, width), BF),
        pltpu.VMEM((2, 2, plan[UPPER][0], width), BF),
        pltpu.VMEM((2, plan[UPPER][0], width), BF),
    ]
    scratch += [pltpu.VMEM((width, cols), BF)] * (layers + 1)
    scratch += [pltpu.VMEM((ff, width), BF)] * (layers + 1)
    scratch += [pltpu.VMEM((width, cols), BF)] * layers
    scratch += [pltpu.VMEM((ff, width), BF)] * layers
    scratch += [pltpu.VMEM((group - 1, rows_in, cols), BF)] * layers
    scratch += [pltpu.VMEM((group - 1, rows_down, width), BF)] * layers
    scratch += [pltpu.VMEM((1 << len(order), r, width), BF) for r, order in plan]
    for r, order in plan:
        count = len(order)
        scratch += [pltpu.VMEM((1 << (count - 1 - t), r, width), BF) for t in range(count)]
        scratch += [pltpu.VMEM((1 << (count - 1 - t), r, width), BF) for t in range(count - 1)]
    scratch += [
        pltpu.SemaphoreType.DMA(dims)
        for dims in [
            (8,), (layers, 2), (group,), (group,), (PLANE, group), (PLANE, group), (PLANE,),
            (PLANE,), (layers, group, 2), (layers, group, 2), (layers, group, 2),
            (layers, group, 2), (group,), (group,), (len(plan), steps), (len(plan), steps),
            (2,), (2,),
        ]
    ]
    found = pl.pallas_call(
        functools.partial(step_kernel, n, group, layers, per_image, capacity, classes, plan),
        out_shape=[
            shape((1, capacity * per_image), F32),
            shape((classes, rows_in), F32),
            shape((layers, rows_in, cols), BF),
            shape((layers, rows_down, width), BF),
            shape((r_in, width), F32),
            shape((plan[DOWN][0], width), F32),
            shape((plan[DOWN + 1][0], width), F32),
            shape((pad, width), F32),
        ],
        in_specs=[hbm()] * 10,
        out_specs=[vmem()] * 8,
        scratch_shapes=scratch,
        compiler_params=pltpu.CompilerParams(
            collective_id=1, has_side_effects=True, vmem_limit_bytes=VMEM_LIMIT
        ),
    )(
        assign.reshape(n), labels, patches.T, patch_embed, positions,
        classifier.transpose(2, 0, 1), client_in, client_down, server_in, server_down,
    )
    loss, gclass, gin, gdown, *sums = found
    cuts = 4 if rows_in % (4 * PAD) == 0 else 1

    def tile(r, c):
        return pl.BlockSpec((1, r // cuts, c), lambda i, j: (i, j, 0))

    def whole(*dims):
        return pl.BlockSpec(dims, lambda i, j: (0, 0))

    gin, gdown, gclass, loss, cin, cdown, embed, pos = pl.pallas_call(
        finish_kernel,
        grid=(layers, cuts),
        out_shape=[
            shape((layers, rows_in, cols), F32),
            shape((layers, rows_down, width), F32),
            shape((classes, rows_in), F32),
            shape((1, capacity * per_image), F32),
            shape((r_in, width), F32),
            shape((own, ff), F32),
            shape((own, patch), F32),
            shape((TOK, own), F32),
        ],
        in_specs=[
            tile(rows_in, cols),
            tile(rows_down, width),
            whole(classes, rows_in),
            whole(1, capacity * per_image),
        ]
        + [whole(*v.shape) for v in sums],
        out_specs=[
            tile(rows_in, cols),
            tile(rows_down, width),
            whole(classes, rows_in),
            whole(1, capacity * per_image),
            whole(r_in, width),
            whole(own, ff),
            whole(own, patch),
            whole(TOK, own),
        ],
        compiler_params=pltpu.CompilerParams(
            dimension_semantics=("arbitrary", "arbitrary"), vmem_limit_bytes=24 * 1024 * 1024
        ),
    )(gin, gdown, gclass, loss, *sums)
    return loss, embed.T, pos, cin.T, cdown.T, gin, gdown, gclass.T


def solution(mesh):
    whole = P()
    in_specs = (
        P("client", None), whole, whole, whole, whole, whole, whole,
        P(None, "client", None), P(None, "client", None), whole,
    )
    out_specs = (
        P("client", None), P(None, "client"), P(None, "client"), P(None, "client"),
        P(None, "client"), P(None, "client", None), P(None, "client", None), P("client", None),
    )
    return jax.shard_map(
        per_device, mesh=mesh, in_specs=in_specs, out_specs=out_specs, check_vma=False
    )
```

time: 132 us -> 89.7 us (0.68)
  Pallas kernels: 102 us -> 81 us
  local copies, waits for them, and re-layouts: 17.7 us -> 7.49 us
  other arithmetic: 9.95 us -> 0 us
    pallas_call x2 -> x1, Pallas kernels: 60.2 us -> 4.27 us  [per_device(): pl.pallas_call(finish_kernel, grid=(layers, cuts), out_shape=[shape((laye...]
    pallas_call x1, Pallas kernels: 41.3 us -> 76.7 us  [per_device(): pl.pallas_call(functools.partial(step_kernel, n, group, layers, per_image...]
    add x3 -> x0, other arithmetic: 7.57 us -> none  [the longest x1 3.06 us: per_device(): parts_down[i].astype(F32)]
    slice x5 -> x0, local copies, waits for them, and re-layouts: 5.07 us -> none  [the longest x1 1.54 us: per_device(): last[:patch]]
    unnamed x15 -> x16, local copies, waits for them, and re-layouts: 11.1 us -> 7.49 us
    transpose x1 -> x0, other arithmetic: 1.57 us -> none  [per_device(): grad_in = jnp.concatenate([sums[0], sums[1][:extra]], axis=0).T]
    transpose x2 -> x0, local copies, waits for them, and re-layouts: 1.56 us -> none  [per_device(): grad_down = down[:-1].transpose(0, 2, 1).reshape(ff, own)]
  transfers between devices with their start and end apart: 5 -> 0, of which waited for: 0 -> 0; matrix products, arithmetic and copies ran while one was open for 17% -> 0% of each run, Pallas kernels for 46% -> 0%
where the time goes in v2:
time: 89.7 us; the launch traced here: 89.3 us
  Pallas kernels  81 us (90%)
  local copies, waits for them, and re-layouts  7.49 us (8%)
    pallas_call x1, Pallas kernels, per_device(): pl.pallas_call(functools.partial(step_kernel, n, group, layers, per_image...  76.7 us
    unnamed x16, local copies, waits for them, and re-layouts  7.49 us
    pallas_call x1, Pallas kernels, per_device(): pl.pallas_call(finish_kernel, grid=(layers, cuts), out_shape=[shape((laye...  4.27 us

profile of v2, /device:TPU:0, one launch (start us, length us, event | category | flops | bytes accessed | tf_op | source)
XLA Modules:
  0.0 89.3 jit_solution(9814226106240885510)
XLA Ops:
  0.6 76.7 %shard_map.161 = (f32[1,16]{1,0:T(1,128)}, f32[10,192]{1,0:T(8,128)}, bf16[2,192,3072]{2,1,0:T(8,128)(2,1)}, bf16[2,768,384]{2,1,0:T(8,128)(2,1)}, f32[96,384]{1...) custom-call(s32[32]{0:T(128)} %bitcast.9, s32[256]{0:T(256)} %refs_1_.1, ...), custom_call_target="tpu_custom_call" | custom-call | tf_op jit(solution)/shard_map/pallas_call | solution.py:827
  77.4 0.0 copy-start
  77.4 1.7 %copy-done = bf16[2,192,3072]{2,1,0:T(8,128)(2,1)S(1)} copy-done((bf16[2,192,3072]{2,1,0:T(8,128)(2,1)S(1)}, bf16[2,192,3072]{2,1,0:T(8,128)(2,1)}, u32[]{:S(2)}) %copy-start) | copy-done | bytes 2359320
  79.0 0.0 copy-start.1
  79.0 1.3 %copy-done.1 = bf16[2,768,384]{2,1,0:T(8,128)(2,1)S(1)} copy-done((bf16[2,768,384]{2,1,0:T(8,128)(2,1)S(1)}, bf16[2,768,384]{2,1,0:T(8,128)(2,1)}, u32[]{:S(2)}) %copy-start.1) | copy-done | bytes 1179672
  80.3 0.0 copy-start.2
  80.3 0.9 %copy-done.2 = f32[96,384]{1,0:T(8,128)S(1)} copy-done((f32[96,384]{1,0:T(8,128)S(1)}, f32[96,384]{1,0:T(8,128)}, u32[]{:S(2)}) %copy-start.2) | copy-done | bytes 147480
  81.2 0.0 copy-start.3
  81.2 0.8 copy-done.3
  82.0 0.0 copy-start.4
  82.0 0.8 copy-done.4
  82.8 0.0 copy-start.5
  82.8 0.7 copy-done.5
  83.6 0.0 copy-start.6
  83.6 0.7 copy-done.6
  84.3 0.0 copy-start.7
  84.3 0.6 copy-done.7
  84.9 4.3 %shard_map.162 = (f32[2,192,3072]{2,1,0:T(8,128)}, f32[2,768,384]{2,1,0:T(8,128)}, f32[10,192]{1,0:T(8,128)}, f32[1,16]{1,0:T(1,128)}, f32[96,384]{1,0:T(8,128)}...) custom-call(bf16[2,192,3072]{2,1,0:T(8,128)(2,1)S(1)} %copy-done, bf16[2,768,384]{2,1,0:T(8,128)(2,1)S(1)} %copy-done.1, ...), custom_call_target="tpu_custom_call" | custom-call | tf_op jit(solution)/shard_map/pallas_call | solution.py:858
Async XLA Ops:
  77.4 1.7 %copy-start = (bf16[2,192,3072]{2,1,0:T(8,128)(2,1)S(1)}, bf16[2,192,3072]{2,1,0:T(8,128)(2,1)}, u32[]{:S(2)}) copy-start(bf16[2,192,3072]{2,1,0:T(8,128)(2,1)} %get-tuple-element.24.near_in) | copy-start | bytes 7077892
  79.0 1.3 %copy-start.1 = (bf16[2,768,384]{2,1,0:T(8,128)(2,1)S(1)}, bf16[2,768,384]{2,1,0:T(8,128)(2,1)}, u32[]{:S(2)}) copy-start(bf16[2,768,384]{2,1,0:T(8,128)(2,1)} %get-tuple-element.25.near_down) | copy-start | bytes 3538948
  80.3 0.9 %copy-start.2 = (f32[96,384]{1,0:T(8,128)S(1)}, f32[96,384]{1,0:T(8,128)}, u32[]{:S(2)}) copy-start(f32[96,384]{1,0:T(8,128)} %get-tuple-element.28.cin_sum) | copy-start | bytes 442372
  81.2 0.8 copy-start.3
  82.0 0.8 copy-start.4
  82.8 0.7 copy-start.5
  83.6 0.7 copy-start.6
  84.3 0.6 copy-start.7

commit v3 on v2

--- a/solution.py
+++ b/solution.py
@@ -212,34 +212,42 @@
     second = [0] + high + low + far
     third = [0] + far + low + high
     top = (r_in // 2 + PAD - 1) // PAD * PAD
-    half = blocks // 2 * pad
     return [
-        (half, first), (blocks * pad - half, second),
+        (pad, first), (pad, second), ((blocks - 2) * pad, third),
         (top, first[:-1]), (r_in - top, second[:-1]),
         (top, first[:-1]), (r_in - top, second[:-1]),
         (pad, third),
     ]
 
 
-DOWN, UPPER, LOWER, LAST = 0, 2, 4, 6
-
-
-def step_kernel(n, group, layers, per_image, capacity, classes, plan, *refs):
+DOWN, UPPER, LOWER, LAST = 0, 3, 5, 7
+
+
+def layout_of(r_in, blocks, pad):
+    sizes = [r_in] + [pad] * (blocks + 1) + [16, 8]
+    starts = [0]
+    for size in sizes:
+        starts.append(starts[-1] + size)
+    return starts
+
+
+def step_kernel(n, group, layers, per_image, capacity, classes, plan, halves, *refs):
     (
         assign_hbm, label_hbm, turned_hbm, embed_hbm, pos_hbm, class_hbm,
         cin_hbm, cdown_hbm, sin_hbm, sdown_hbm,
     ) = refs[:10]
     refs = refs[10:]
-    loss_ref, gclass_ref, gin_sum, gdown_sum, cin_sum, down_first, down_second, last_sum = refs[:8]
-    refs = refs[8:]
+    gin_sum, gdown_sum, rest = refs[:3]
+    refs = refs[3:]
     (
         assign_ref, label_ref, turned_ref, embed_ref, pos_ref, class_ref,
-        patch_ref, column, pack, got_slots, slots_ref,
-        first_u, first_s, qkv, probs, att, second_u, second_s, hidden,
+        slots_ref, first_u, first_s, qkv, probs, att, second_u, second_s, hidden,
         slope, dqkv, gcur,
         gclass_own, gclass_got, joined, joined_got,
-    ) = refs[:26]
-    refs = refs[26:]
+    ) = refs[:22]
+    refs = refs[22:]
+    patch_ref, column, refs = refs[:halves], refs[halves : 2 * halves], refs[2 * halves :]
+    pack, got_slots, refs = refs[:halves], refs[halves : 2 * halves], refs[2 * halves :]
     wbuf, dbuf, refs = refs[: layers + 1], refs[layers + 1 : 2 * layers + 2], refs[2 * layers + 2 :]
     gin, gdown, refs = refs[:layers], refs[layers : 2 * layers], refs[2 * layers :]
     gin_got, gdown_got, refs = refs[:layers], refs[layers : 2 * layers], refs[2 * layers :]
@@ -253,7 +261,7 @@
         refs = refs[2 * count - 1 :]
     (
         load_sem, own_sem, near_send, near_recv, far_send, far_recv, flat_send, flat_recv,
-        w_send, w_recv, g_send, g_recv, c_send, c_recv, r_send, r_recv, j_send, j_recv,
+        w_send, w_recv, g_send, g_recv, c_send, c_recv, r_send, r_recv, j_send, j_recv, o_sem,
     ) = refs
     steps = bits_of(n)
     me = lax.axis_index("client")
@@ -265,6 +273,7 @@
     rows_down = sdown_hbm.shape[1]
     rows, width = gcur.shape
     ff = dbuf[0].shape[0]
+    rows_at = layout_of(wbuf[0].shape[1] // n, ff // width, pad_of(width // n))
 
     loads = [
         pltpu.make_async_copy(source, target, load_sem.at[i])
@@ -306,25 +315,28 @@
             device_id=(peer,), device_id_type=MESH,
         )
 
-    def near(i):
+    def near(h, i):
         to = lax.rem(rank + i, group)
         return remote(
-            patch_ref.at[to], column.at[line, rank], near_send.at[i], near_recv.at[i], near_peer(i)
-        )
-
-    def far(i, j):
+            patch_ref[h].at[to], column[h].at[line, rank], near_send.at[h, i], near_recv.at[h, i],
+            near_peer(i),
+        )
+
+    def far(h, i, j):
         if j == 0:
-            source, member = patch_ref.at[rank], rank
+            source, member = patch_ref[h].at[rank], rank
         else:
             member = lax.rem(rank + group - j, group)
-            source = column.at[line, member]
+            source = column[h].at[line, member]
         return remote(
-            source, column.at[line, member], far_send.at[i, j], far_recv.at[i, j], far_peer(i)
-        )
-
-    def flat(i):
+            source, column[h].at[line, member], far_send.at[h, i, j], far_recv.at[h, i, j],
+            far_peer(i),
+        )
+
+    def flat(h, i):
         return remote(
-            pack.at[i], got_slots.at[spot], flat_send.at[i], flat_recv.at[i], flat_peer(i)
+            pack[h].at[i], got_slots[h].at[spot], flat_send.at[h, i], flat_recv.at[h, i],
+            flat_peer(i),
         )
 
     def weight_in(layer, i):
@@ -369,22 +381,30 @@
         own_in(layer).start()
         own_down(layer).start()
     loads[0].wait()
-    patch_ref[...] = turned_ref[...].astype(F32).T.astype(BF).reshape(patch_ref.shape)
+    turned = turned_ref[...].astype(F32).T.astype(BF)
+    piece = turned.shape[0] // group
+    size = piece // halves
+    for i in range(group):
+        for h in range(halves):
+            lo = i * piece + h * size
+            patch_ref[h][i] = turned[lo : lo + size]
     pl.semaphore_wait(barrier, len(peers))
 
-    for i in range(1, group):
-        near(i).start()
-    for i in range(1, PLANE):
-        far(i, 0).start()
+    for h in range(halves):
+        for i in range(1, group):
+            near(h, i).start()
+        for i in (2, 1, 3):
+            far(h, i, 0).start()
     for layer in range(layers):
         for i in range(1, group):
             weight_in(layer, i).start()
             weight_down(layer, i).start()
-    for j in range(1, group):
-        near(j).wait_recv()
-        for i in range(1, PLANE):
-            far(i, j).start()
-    column[line, rank] = patch_ref[rank]
+    for h in range(halves):
+        for j in range(1, group):
+            near(h, j).wait_recv()
+            for i in (2, 1, 3):
+                far(h, i, j).start()
+        column[h][line, rank] = patch_ref[h][rank]
 
     targets = [line * PLANE + lax.rem(spot + i, PLANE) for i in range(PLANE)]
     loads[1].wait()
@@ -423,28 +443,29 @@
     chosen = lax.broadcasted_iota(jnp.int32, every.shape, 1) == shard
     cls = jnp.sum(jnp.where(chosen, every, 0.0), axis=1).astype(BF)
 
-    for i in range(1, PLANE):
-        for j in range(group):
-            far(i, j).wait_recv()
-
-    def pick(c):
+    def pick(h, c):
         home = c // group
-        return column[home // PLANE, c % group]
-
-    for i in range(1, PLANE):
+        return column[h][home // PLANE, c % group]
+
+    for h in range(halves):
+        for i in range(1, PLANE):
+            for j in range(group):
+                far(h, i, j).wait_recv()
+        for i in (3, 1, 2):
+            for k in range(capacity):
+                pack[h][i, k] = pick(h, table[i][1][k])
+            flat(h, i).start()
         for k in range(capacity):
-            pack[i, k] = pick(table[i][1][k])
-        flat(i).start()
-    for k in range(capacity):
-        got_slots[spot, k] = pick(slots[k])
+            got_slots[h][spot, k] = pick(h, slots[k])
     for c in (3, 4, 6, 7):
         loads[c].wait()
-    for i in range(1, PLANE):
-        flat(i).wait_recv()
-    piece = patch_ref.shape[1]
-    for k in range(capacity):
-        home = slots[k] // group
-        slots_ref[k * piece : (k + 1) * piece, :] = got_slots[home % PLANE, k]
+    for h in range(halves):
+        for i in range(1, PLANE):
+            flat(h, i).wait_recv()
+        for k in range(capacity):
+            home = slots[k] // group
+            lo = k * piece + h * size
+            slots_ref[lo : lo + size, :] = got_slots[h][home % PLANE, k]
 
     x = mm(slots_ref[...], embed_ref[...])
     pos = pos_ref[...].astype(F32)
@@ -488,7 +509,9 @@
         lax.broadcasted_iota(jnp.int32, (images, images), 0)
         == lax.broadcasted_iota(jnp.int32, (images, images), 1)
     )
-    loss_ref[...] = jnp.sum(jnp.where(eye, loss, 0.0), axis=0, keepdims=True)
+    rest[rows_at[-2] : rows_at[-2] + 1, :images] = jnp.sum(
+        jnp.where(eye, loss, 0.0), axis=0, keepdims=True
+    )
     dlog = ((e / total - hot) * full).astype(BF)
     gclass_own[...] = mm_tn(dlog, pooled).astype(BF)
     for i in range(1, group):
@@ -511,9 +534,10 @@
         gcur[...] = block_backward(
             gcur[...], wbuf[deep], dbuf[deep], *saved(deep), dqkv, put_in, put_down,
         )
-        for i in range(1, group):
-            grad_down(layer, i).start()
-            grad_in(layer, i).start()
+        if layer:
+            for i in range(1, group):
+                grad_down(layer, i).start()
+                grad_in(layer, i).start()
 
     def peer_of(bit):
         return me + (1 << bit) - 2 * (1 << bit) * (me // (1 << bit) % 2)
@@ -544,15 +568,12 @@
         )
 
     def store_final(c, value):
-        if c == LAST:
-            last_sum[...] = value
-        elif c == DOWN:
-            down_first[...] = value
-        elif c == DOWN + 1:
-            down_second[...] = value
+        if c == LAST or c < UPPER:
+            lo = rows_at[-4] if c == LAST else rows_at[1 + c]
+            rest[lo : lo + value.shape[0], :] = value
         else:
             side = 1 if c < LOWER else 0
-            joined[c % 2, side, : value.shape[0]] = value.astype(BF)
+            joined[(c - UPPER) % 2, side, : value.shape[0]] = value.astype(BF)
 
     progress = [0] * chains
 
@@ -605,34 +626,36 @@
         spread = mm(gb, spread_to).astype(BF)
         for q in range(ff // width):
             part = mm_tn(spread, h[:, q * width : (q + 1) * width]).astype(BF)
-            c = DOWN if q * pad < plan[DOWN][0] else DOWN + 1
-            lo = q * pad if c == DOWN else q * pad - plan[DOWN][0]
+            c = DOWN + min(q, 2)
+            lo = max(q - 2, 0) * pad
             for j in range(n):
                 packs[c][place_of(j, plan[c][1]), lo : lo + pad] = part[j * pad : (j + 1) * pad]
 
     def after(stage):
         if stage == 0:
-            copy(DOWN, 0).start()
-            copy(DOWN + 1, 0).start()
+            for c in range(DOWN, UPPER):
+                copy(c, 0).start()
         elif stage == 1:
-            copy(UPPER, 0).start()
-            copy(UPPER + 1, 0).start()
-            advance(DOWN)
-            advance(DOWN + 1)
-        elif stage == 2:
-            advance(UPPER)
-            advance(UPPER + 1)
+            for c in range(UPPER, LOWER):
+                copy(c, 0).start()
+            for c in (DOWN + 2, DOWN, DOWN + 1):
+                advance(c)
         elif stage == 3:
-            advance(DOWN)
-            advance(DOWN + 1)
-        else:
-            copy(LOWER, 0).start()
-            copy(LOWER + 1, 0).start()
+            for c in range(UPPER, LOWER):
+                advance(c)
+        elif stage == 4:
+            for c in range(LOWER, LAST):
+                copy(c, 0).start()
+            for i in range(1, group):
+                grad_down(0, i).start()
+                grad_in(0, i).start()
 
     dx = block_backward(
         gcur[...].astype(BF).astype(F32), wbuf[0], dbuf[0], *saved(0), dqkv,
         put_in, put_down, after,
     )
+    for c in range(LOWER, LAST):
+        advance(c)
     spread = mm(dx.astype(BF), spread_to).astype(BF)
     patch = slots_ref.shape[1]
     embed_part = mm_tn(spread, slots_ref[...]).astype(BF)
@@ -644,6 +667,14 @@
         packs[LAST][at, :, width - LANES :] = pos_part[j * pad : (j + 1) * pad]
     copy(LAST, 0).start()
 
+    def gin_out(layer):
+        return pltpu.make_async_copy(gin_got[layer].at[0], gin_sum.at[layer], o_sem.at[layer, 0])
+
+    def gdown_out(layer):
+        return pltpu.make_async_copy(
+            gdown_got[layer].at[0], gdown_sum.at[layer], o_sem.at[layer, 1]
+        )
+
     def add_layer(layer):
         for i in range(1, group):
             grad_down(layer, i).wait_recv()
@@ -652,25 +683,29 @@
         whole = gin[layer][pl.ds(start, rows_in)].astype(F32)
         for i in range(1, group):
             whole = whole + gin_got[layer][i - 1].astype(F32)
-        gin_sum[layer] = whole.astype(BF)
+        gin_got[layer][0] = whole.astype(BF)
+        gin_out(layer).start()
         start = rank * rows_down
         whole = gdown[layer][pl.ds(start, rows_down)].astype(F32)
         for i in range(1, group):
             whole = whole + gdown_got[layer][i - 1].astype(F32)
-        gdown_sum[layer] = whole.astype(BF)
+        gdown_got[layer][0] = whole.astype(BF)
+        gdown_out(layer).start()
+
+    def finished(c):
+        return progress[c] == len(plan[c][1])
 
     rounds = 0
-    while any(progress[c] < len(plan[c][1]) for c in range(chains)):
-        for c in (LOWER, LOWER + 1, UPPER, UPPER + 1, LAST, DOWN, DOWN + 1):
-            done = progress[c] == len(plan[c][1])
+    started = [False, False]
+    while not all(finished(c) for c in range(chains)):
+        for c in (2, 0, 1, UPPER, UPPER + 1, LAST, LOWER, LOWER + 1):
             advance(c)
-            if LOWER <= c < LAST and not done and progress[c] == len(plan[c][1]):
-                other = c - LOWER + UPPER
-                while progress[other] < len(plan[other][1]):
-                    advance(other)
-                join(c - LOWER).start()
-        if rounds < layers:
-            add_layer(layers - 1 - rounds)
+            for k in range(2):
+                if finished(UPPER + k) and finished(LOWER + k) and not started[k]:
+                    started[k] = True
+                    join(k).start()
+        if 0 < rounds <= layers:
+            add_layer(layers - rounds)
         rounds += 1
     for i in range(1, group):
         grad_class(i).wait_recv()
@@ -680,57 +715,81 @@
     kept = both[:, :rows_in]
     for i in range(1, group):
         kept = jnp.where(rank == i, both[:, i * rows_in : (i + 1) * rows_in], kept)
-    gclass_ref[...] = kept
+    rest[rows_at[-3] : rows_at[-3] + classes, :rows_in] = kept
     lo = 0
     for c in range(2):
         join(c).wait_recv()
         take = plan[UPPER + c][0]
-        cin_sum[lo : lo + take, :] = (
+        rest[lo : lo + take, :] = (
             joined[c, mine(steps - 1), :take].astype(F32) + joined_got[c, :take].astype(F32)
         )
         lo += take
 
+    for h in range(halves):
+        for i in range(1, group):
+            near(h, i).wait_send()
+        for i in range(1, PLANE):
+            flat(h, i).wait_send()
+            for j in range(group):
+                far(h, i, j).wait_send()
     for i in range(1, group):
-        near(i).wait_send()
         grad_class(i).wait_send()
         for layer in range(layers):
             weight_in(layer, i).wait_send()
             weight_down(layer, i).wait_send()
             grad_in(layer, i).wait_send()
             grad_down(layer, i).wait_send()
-    for i in range(1, PLANE):
-        flat(i).wait_send()
-        for j in range(group):
-            far(i, j).wait_send()
     for c in range(chains):
         for t in range(len(plan[c][1])):
             copy(c, t).wait_send()
     for c in range(2):
         join(c).wait_send()
+    for layer in range(layers):
+        gin_out(layer).wait()
+        gdown_out(layer).wait()
 
 
 def finish_kernel(
-    near_in, near_down, class_ref, loss_in, cin_sum, down_first, down_second, last_sum,
-    gin_ref, gdown_ref, gclass_ref, loss_ref, cin_ref, cdown_ref, embed_ref, pos_ref,
+    cuts, rows_at, gin_hbm, gdown_hbm, rest_hbm,
+    gin_out, gdown_out, gclass_ref, loss_ref, cin_ref, cdown_ref, embed_ref, pos_ref,
+    gin_near, gdown_near, rest, gin_wide, gdown_wide, in_sem, out_sem, rest_sem,
 ):
-    gin_ref[...] = near_in[...].astype(F32)
-    gdown_ref[...] = near_down[...].astype(F32)
-
-    @pl.when((pl.program_id(0) == 0) & (pl.program_id(1) == 0))
-    def _():
-        gclass_ref[...] = class_ref[...]
-        loss_ref[...] = loss_in[...]
-        cin_ref[...] = cin_sum[...]
-        own, width = cdown_ref.shape[0], cin_sum.shape[1]
-        pad = pad_of(own)
-        q = 0
-        for part in (down_first, down_second):
-            for lo in range(0, part.shape[0], pad):
-                cdown_ref[:, q * width : (q + 1) * width] = part[lo : lo + pad, :][:own]
-                q += 1
-        last = last_sum[...]
-        embed_ref[...] = last[:own, : embed_ref.shape[1]]
-        pos_ref[...] = last[:, width - LANES :].T[:TOK, :own]
+    layers, rows_in, rows_down = gin_hbm.shape[0], gin_hbm.shape[1], gdown_hbm.shape[1]
+    pieces = []
+    for layer in range(layers):
+        for j in range(cuts):
+            for source, near, wide, out, size, kind in (
+                (gin_hbm, gin_near, gin_wide, gin_out, rows_in // cuts, 0),
+                (gdown_hbm, gdown_near, gdown_wide, gdown_out, rows_down // cuts, 1),
+            ):
+                at = (layer, pl.ds(j * size, size))
+                pieces.append((
+                    pltpu.make_async_copy(source.at[at], near.at[at], in_sem.at[layer, j, kind]),
+                    pltpu.make_async_copy(wide.at[at], out.at[at], out_sem.at[layer, j, kind]),
+                    near, wide, at,
+                ))
+    load = pltpu.make_async_copy(rest_hbm, rest, rest_sem)
+    load.start()
+    for piece in pieces:
+        piece[0].start()
+    for arrive, leave, near, wide, at in pieces:
+        arrive.wait()
+        wide[at] = near[at].astype(F32)
+        leave.start()
+    load.wait()
+    cin_ref[...] = rest[: cin_ref.shape[0], :]
+    own, width = cdown_ref.shape[0], rest.shape[1]
+    for q in range(cdown_ref.shape[1] // width):
+        lo = rows_at[1 + q]
+        cdown_ref[:, q * width : (q + 1) * width] = rest[lo : lo + own, :]
+    last = rest[rows_at[-4] : rows_at[-3], :]
+    embed_ref[...] = last[:own, : embed_ref.shape[1]]
+    pos_ref[...] = last[:, width - LANES :].T[:TOK, :own]
+    classes, shared = gclass_ref.shape
+    gclass_ref[...] = rest[rows_at[-3] : rows_at[-3] + classes, :shared]
+    loss_ref[...] = rest[rows_at[-2] : rows_at[-2] + 1, : loss_ref.shape[1]]
+    for piece in pieces:
+        piece[1].wait()
 
 
 def vmem():
@@ -761,6 +820,7 @@
     rows_down = server_down.shape[1]
     classes = classifier.shape[2]
     piece = rows // group
+    halves = 2 if piece % (2 * PAD) == 0 else 1
     per_image = IMG // group
     capacity = SLOTS * group
     s_rows = capacity * piece
@@ -770,6 +830,7 @@
     pad = pad_of(own)
     plan = chain_plan(n, r_in, ff // width, pad)
     shards = classifier.shape[0]
+    rows_at = layout_of(r_in, ff // width, pad)
     per = LANES // (width // HEADS)
     spaces = [
         ((s_rows, width), BF),
@@ -789,10 +850,6 @@
         pltpu.VMEM((patch, width), BF),
         pltpu.VMEM((TOK, width), BF),
         pltpu.VMEM((classes, shards, width), BF),
-        pltpu.VMEM((group, piece, patch), BF),
-        pltpu.VMEM((PLANE, group, piece, patch), BF),
-        pltpu.VMEM((PLANE, capacity, piece, patch), BF),
-        pltpu.VMEM((PLANE, capacity, piece, patch), BF),
         pltpu.VMEM((s_rows, patch), BF),
     ]
     scratch += [pltpu.VMEM((layers + 1,) + dims, kind) for dims, kind in spaces]
@@ -804,6 +861,8 @@
         pltpu.VMEM((2, 2, plan[UPPER][0], width), BF),
         pltpu.VMEM((2, plan[UPPER][0], width), BF),
     ]
+    for dims in ((group,), (PLANE, group), (PLANE, capacity), (PLANE, capacity)):
+        scratch += [pltpu.VMEM(dims + (piece // halves, patch), BF)] * halves
     scratch += [pltpu.VMEM((width, cols), BF)] * (layers + 1)
     scratch += [pltpu.VMEM((ff, width), BF)] * (layers + 1)
     scratch += [pltpu.VMEM((width, cols), BF)] * layers
@@ -818,26 +877,23 @@
     scratch += [
         pltpu.SemaphoreType.DMA(dims)
         for dims in [
-            (8,), (layers, 2), (group,), (group,), (PLANE, group), (PLANE, group), (PLANE,),
-            (PLANE,), (layers, group, 2), (layers, group, 2), (layers, group, 2),
+            (8,), (layers, 2), (halves, group), (halves, group), (halves, PLANE, group),
+            (halves, PLANE, group), (halves, PLANE), (halves, PLANE), (layers, group, 2), (layers, group, 2), (layers, group, 2),
             (layers, group, 2), (group,), (group,), (len(plan), steps), (len(plan), steps),
-            (2,), (2,),
+            (2,), (2,), (layers, 2),
         ]
     ]
     found = pl.pallas_call(
-        functools.partial(step_kernel, n, group, layers, per_image, capacity, classes, plan),
+        functools.partial(
+            step_kernel, n, group, layers, per_image, capacity, classes, plan, halves
+        ),
         out_shape=[
-            shape((1, capacity * per_image), F32),
-            shape((classes, rows_in), F32),
             shape((layers, rows_in, cols), BF),
             shape((layers, rows_down, width), BF),
-            shape((r_in, width), F32),
-            shape((plan[DOWN][0], width), F32),
-            shape((plan[DOWN + 1][0], width), F32),
-            shape((pad, width), F32),
+            shape((rows_at[-1], width), F32),
         ],
         in_specs=[hbm()] * 10,
-        out_specs=[vmem()] * 8,
+        out_specs=[hbm(), hbm(), vmem()],
         scratch_shapes=scratch,
         compiler_params=pltpu.CompilerParams(
             collective_id=1, has_side_effects=True, vmem_limit_bytes=VMEM_LIMIT
@@ -846,18 +902,9 @@
         assign.reshape(n), labels, patches.T, patch_embed, positions,
         classifier.transpose(2, 0, 1), client_in, client_down, server_in, server_down,
     )
-    loss, gclass, gin, gdown, *sums = found
     cuts = 4 if rows_in % (4 * PAD) == 0 else 1
-
-    def tile(r, c):
-        return pl.BlockSpec((1, r // cuts, c), lambda i, j: (i, j, 0))
-
-    def whole(*dims):
-        return pl.BlockSpec(dims, lambda i, j: (0, 0))
-
     gin, gdown, gclass, loss, cin, cdown, embed, pos = pl.pallas_call(
-        finish_kernel,
-        grid=(layers, cuts),
+        functools.partial(finish_kernel, cuts, rows_at),
         out_shape=[
             shape((layers, rows_in, cols), F32),
             shape((layers, rows_down, width), F32),
@@ -868,27 +915,20 @@
             shape((own, patch), F32),
             shape((TOK, own), F32),
         ],
-        in_specs=[
-            tile(rows_in, cols),
-            tile(rows_down, width),
-            whole(classes, rows_in),
-            whole(1, capacity * per_image),
-        ]
-        + [whole(*v.shape) for v in sums],
-        out_specs=[
-            tile(rows_in, cols),
-            tile(rows_down, width),
-            whole(classes, rows_in),
-            whole(1, capacity * per_image),
-            whole(r_in, width),
-            whole(own, ff),
-            whole(own, patch),
-            whole(TOK, own),
+        in_specs=[hbm()] * 3,
+        out_specs=[hbm()] * 2 + [vmem()] * 6,
+        scratch_shapes=[
+            pltpu.VMEM((layers, rows_in, cols), BF),
+            pltpu.VMEM((layers, rows_down, width), BF),
+            pltpu.VMEM((rows_at[-1], width), F32),
+            pltpu.VMEM((layers, rows_in, cols), F32),
+            pltpu.VMEM((layers, rows_down, width), F32),
+            pltpu.SemaphoreType.DMA((layers, cuts, 2)),
+            pltpu.SemaphoreType.DMA((layers, cuts, 2)),
+            pltpu.SemaphoreType.DMA,
         ],
-        compiler_params=pltpu.CompilerParams(
-            dimension_semantics=("arbitrary", "arbitrary"), vmem_limit_bytes=24 * 1024 * 1024
-        ),
-    )(gin, gdown, gclass, loss, *sums)
+        compiler_params=pltpu.CompilerParams(vmem_limit_bytes=24 * 1024 * 1024),
+    )(*found)
     return loss, embed.T, pos, cin.T, cdown.T, gin, gdown, gclass.T
 
 

time: 89.7 us -> 81.8 us (0.912)
  Pallas kernels: 81 us -> 76.9 us
  local copies, waits for them, and re-layouts: 7.49 us -> 3.89 us
    pallas_call x1, Pallas kernels: 76.7 us -> 70.9 us  [per_device(): pl.pallas_call(functools.partial(step_kernel, n, group, layers, per_image...]
    unnamed x16 -> x6, local copies, waits for them, and re-layouts: 7.49 us -> 3.89 us
    pallas_call x1, Pallas kernels: 4.27 us -> 5.99 us  [per_device(): pl.pallas_call(functools.partial(finish_kernel, cuts, rows_at), out_shape...]
where the time goes in v3:
time: 81.8 us; the launch traced here: 81.6 us
  Pallas kernels  76.9 us (94%)
  local copies, waits for them, and re-layouts  3.89 us (5%)
  between operations  0.82 us (1%)
    pallas_call x1, Pallas kernels, per_device(): pl.pallas_call(functools.partial(step_kernel, n, group, layers, per_image...  70.9 us
    pallas_call x1, Pallas kernels, per_device(): pl.pallas_call(functools.partial(finish_kernel, cuts, rows_at), out_shape...  5.99 us
    unnamed x6, local copies, waits for them, and re-layouts  3.89 us

profile of v3, /device:TPU:0, one launch (start us, length us, event | category | flops | bytes accessed | tf_op | source)
XLA Modules:
  0.0 81.6 jit_solution(13349591948299704468)
XLA Ops:
  0.6 70.9 %shard_map.161 = (bf16[2,192,3072]{2,1,0:T(8,128)(2,1)}, bf16[2,768,384]{2,1,0:T(8,128)(2,1)}, f32[200,384]{1,0:T(8,128)}) custom-call(s32[32]{0:T(128)} %bitcast.9, s32[256]{0:T(256)} %refs_1_.1, bf16[192,128]{1,0:T(8,128)(2,1)} %bitcast.8, bf16[192,384]{1,0:T(8,128)(2,1)} %refs_3_.1, bf16[16,384]{1,0:T(8,128)(2,1)} %refs_4_.1, ...), custom_call_target="tpu_custom_call" | custom-call | tf_op jit(solution)/shard_map/pallas_call | solution.py:886
  71.6 0.0 copy-start
  71.6 1.7 %copy-done = bf16[2,192,3072]{2,1,0:T(8,128)(2,1)S(1)} copy-done((bf16[2,192,3072]{2,1,0:T(8,128)(2,1)S(1)}, bf16[2,192,3072]{2,1,0:T(8,128)(2,1)}, u32[]{:S(2)}) %copy-start) | copy-done | bytes 2359320
  73.2 0.0 copy-start.1
  73.2 1.3 %copy-done.1 = bf16[2,768,384]{2,1,0:T(8,128)(2,1)S(1)} copy-done((bf16[2,768,384]{2,1,0:T(8,128)(2,1)S(1)}, bf16[2,768,384]{2,1,0:T(8,128)(2,1)}, u32[]{:S(2)}) %copy-start.1) | copy-done | bytes 1179672
  74.5 0.0 copy-start.2
  74.5 1.0 %copy-done.2 = f32[200,384]{1,0:T(8,128)S(1)} copy-done((f32[200,384]{1,0:T(8,128)S(1)}, f32[200,384]{1,0:T(8,128)}, u32[]{:S(2)}) %copy-start.2) | copy-done | bytes 307224
  75.5 6.0 %shard_map.162 = (f32[2,192,3072]{2,1,0:T(8,128)}, f32[2,768,384]{2,1,0:T(8,128)}, f32[10,192]{1,0:T(8,128)}, f32[1,16]{1,0:T(1,128)}, f32[96,384]{1,0:T(8,128)}...) custom-call(bf16[2,192,3072]{2,1,0:T(8,128)(2,1)S(1)} %copy-done, bf16[2,768,384]{2,1,0:T(8,128)(2,1)S(1)} %copy-done.1, ...), custom_call_target="tpu_custom_call" | custom-call | tf_op jit(solution)/shard_map/pallas_call | solution.py:906
Async XLA Ops:
  71.6 1.7 %copy-start = (bf16[2,192,3072]{2,1,0:T(8,128)(2,1)S(1)}, bf16[2,192,3072]{2,1,0:T(8,128)(2,1)}, u32[]{:S(2)}) copy-start(bf16[2,192,3072]{2,1,0:T(8,128)(2,1)} %get-tuple-element.19.gin_hbm) | copy-start | bytes 7077892
  73.2 1.3 %copy-start.1 = (bf16[2,768,384]{2,1,0:T(8,128)(2,1)S(1)}, bf16[2,768,384]{2,1,0:T(8,128)(2,1)}, u32[]{:S(2)}) copy-start(bf16[2,768,384]{2,1,0:T(8,128)(2,1)} %get-tuple-element.20.gdown_hbm) | copy-start | bytes 3538948
  74.5 1.0 %copy-start.2 = (f32[200,384]{1,0:T(8,128)S(1)}, f32[200,384]{1,0:T(8,128)}, u32[]{:S(2)}) copy-start(f32[200,384]{1,0:T(8,128)} %get-tuple-element.21.rest_hbm) | copy-start | bytes 921604

commit v4 on v3

--- a/solution.py
+++ b/solution.py
@@ -638,6 +638,7 @@
         elif stage == 1:
             for c in range(UPPER, LOWER):
                 copy(c, 0).start()
+        elif stage == 2:
             for c in (DOWN + 2, DOWN, DOWN + 1):
                 advance(c)
         elif stage == 3:
@@ -927,7 +928,7 @@
             pltpu.SemaphoreType.DMA((layers, cuts, 2)),
             pltpu.SemaphoreType.DMA,
         ],
-        compiler_params=pltpu.CompilerParams(vmem_limit_bytes=24 * 1024 * 1024),
+        compiler_params=pltpu.CompilerParams(vmem_limit_bytes=67000000),
     )(*found)
     return loss, embed.T, pos, cin.T, cdown.T, gin, gdown, gclass.T
 

time: 81.8 us -> 76.6 us (0.936)
  local copies, waits for them, and re-layouts: 3.89 us -> 0 us
  Pallas kernels: 76.9 us -> 75.6 us
    unnamed x6 -> x0, local copies, waits for them, and re-layouts: 3.89 us -> none
    pallas_call x1, Pallas kernels: 5.99 us -> 4.88 us  [per_device(): pl.pallas_call(functools.partial(finish_kernel, cuts, rows_at), out_shape...]
where the time goes in v4:
time: 76.6 us; the launch traced here: 76.4 us
  Pallas kernels  75.6 us (99%)
  between operations  0.81 us (1%)
    pallas_call x1, Pallas kernels, per_device(): pl.pallas_call(functools.partial(step_kernel, n, group, layers, per_image...  70.8 us
    pallas_call x1, Pallas kernels, per_device(): pl.pallas_call(functools.partial(finish_kernel, cuts, rows_at), out_shape...  4.88 us

profile of v4, /device:TPU:0, one launch (start us, length us, event | category | flops | bytes accessed | tf_op | source)
XLA Modules:
  0.0 76.4 jit_solution(10028008626750650737)
XLA Ops:
  0.6 70.8 %shard_map.161 = (bf16[2,192,3072]{2,1,0:T(8,128)(2,1)}, bf16[2,768,384]{2,1,0:T(8,128)(2,1)}, f32[200,384]{1,0:T(8,128)}) custom-call(s32[32]{0:T(128)} %bitcast.9, s32[256]{0:T(256)} %refs_1_.1, bf16[192,128]{1,0:T(8,128)(2,1)} %bitcast.8, bf16[192,384]{1,0:T(8,128)(2,1)} %refs_3_.1, bf16[16,384]{1,0:T(8,128)(2,1)} %refs_4_.1, ...), custom_call_target="tpu_custom_call" | custom-call | tf_op jit(solution)/shard_map/pallas_call | solution.py:887
  71.4 4.9 %shard_map.162 = (f32[2,192,3072]{2,1,0:T(8,128)}, f32[2,768,384]{2,1,0:T(8,128)}, f32[10,192]{1,0:T(8,128)}, f32[1,16]{1,0:T(1,128)}, f32[96,384]{1,0:T(8,128)}...) custom-call(bf16[2,192,3072]{2,1,0:T(8,128)(2,1)} %get-tuple-element.19.gin_hbm, ...), custom_call_target="tpu_custom_call" | custom-call | tf_op jit(solution)/shard_map/pallas_call | solution.py:907

commit v5 on v4

--- a/solution.py
+++ b/solution.py
@@ -705,8 +705,8 @@
                 if finished(UPPER + k) and finished(LOWER + k) and not started[k]:
                     started[k] = True
                     join(k).start()
-        if 0 < rounds <= layers:
-            add_layer(layers - rounds)
+        if rounds < layers:
+            add_layer(layers - 1 - rounds)
         rounds += 1
     for i in range(1, group):
         grad_class(i).wait_recv()

time: 76.6 us -> 76.6 us (level)
  no operation moved by 1% of the time
where the time goes in v5:
time: 76.6 us; the launch traced here: 76.4 us
  Pallas kernels  75.6 us (99%)
  between operations  0.81 us (1%)
    pallas_call x1, Pallas kernels, per_device(): pl.pallas_call(functools.partial(step_kernel, n, group, layers, per_image...  70.8 us
    pallas_call x1, Pallas kernels, per_device(): pl.pallas_call(functools.partial(finish_kernel, cuts, rows_at), out_shape...  4.88 us

profile of v5, /device:TPU:0, one launch (start us, length us, event | category | flops | bytes accessed | tf_op | source)
XLA Modules:
  0.0 76.4 jit_solution(11364660755498319757)
XLA Ops:
  0.6 70.8 %shard_map.161 = (bf16[2,192,3072]{2,1,0:T(8,128)(2,1)}, bf16[2,768,384]{2,1,0:T(8,128)(2,1)}, f32[200,384]{1,0:T(8,128)}) custom-call(s32[32]{0:T(128)} %bitcast.9, s32[256]{0:T(256)} %refs_1_.1, bf16[192,128]{1,0:T(8,128)(2,1)} %bitcast.8, bf16[192,384]{1,0:T(8,128)(2,1)} %refs_3_.1, bf16[16,384]{1,0:T(8,128)(2,1)} %refs_4_.1, ...), custom_call_target="tpu_custom_call" | custom-call | tf_op jit(solution)/shard_map/pallas_call | solution.py:887
  71.4 4.9 %shard_map.162 = (f32[2,192,3072]{2,1,0:T(8,128)}, f32[2,768,384]{2,1,0:T(8,128)}, f32[10,192]{1,0:T(8,128)}, f32[1,16]{1,0:T(1,128)}, f32[96,384]{1,0:T(8,128)}...) custom-call(bf16[2,192,3072]{2,1,0:T(8,128)(2,1)} %get-tuple-element.19.gin_hbm, ...), custom_call_target="tpu_custom_call" | custom-call | tf_op jit(solution)/shard_map/pallas_call | solution.py:907
